TPU v7x, 32 devices: a whole 2x2x4 slice. The times are simulated.
32 devices in a mesh: leaf: 8 (over z, y), grid: 4 (over x, core).
Axes of the slice: x: 2, y: 2, z: 4, core: 2. Of those that a mesh axis runs over, the one named last changes fastest.
Arguments:
- source_leaf: float32 [8, 4096], P(None, ('leaf', 'grid')), may hold values from -6 to 6
- block_leaf: float32 [4096, 128], P(('leaf', 'grid')), may hold values from -0.5 to 0.5
- expand_leaf: float32 [4096, 128], P(('leaf', 'grid')), may hold values from -0.5 to 0.5
- basis_leaf: float32 [4096, 256], P(('leaf', 'grid')), may hold values from -0.25 to 0.25
- pivot_leaf: float32 [4096], P(('leaf', 'grid')), may hold values from -2 to 2
- couple_leaf: float32 [8192, 128], P(('leaf', 'grid')), may hold values from -0.5 to 0.5
- ranks_leaf: int32 [8, 2], replicated, may hold values from 32 to 128
- targets_leaf: int32 [8192], P(('leaf', 'grid')), may hold values from 0 to 2047, as said below
- source_middle: float32 [8, 4096], P(None, ('leaf', 'grid')), may hold values from -6 to 6
- block_middle: float32 [4096, 128], P(('leaf', 'grid')), may hold values from -0.5 to 0.5
- expand_middle: float32 [4096, 128], P(('leaf', 'grid')), may hold values from -0.5 to 0.5
- basis_middle: float32 [4096, 256], P(('leaf', 'grid')), may hold values from -0.1875 to 0.1875
- pivot_middle: float32 [4096], P(('leaf', 'grid')), may hold values from -2 to 2
- couple_middle: float32 [4096, 128], P(('leaf', 'grid')), may hold values from -0.5 to 0.5
- ranks_middle: int32 [4, 2], replicated, may hold values from 32 to 128
- targets_middle: int32 [4096], P(('leaf', 'grid')), may hold values from 0 to 4095, as said below
- source_upper: float32 [8, 4096], P(None, ('leaf', 'grid')), may hold values from -6 to 6
- block_upper: float32 [4096, 128], P(('leaf', 'grid')), may hold values from -0.5 to 0.5
- expand_upper: float32 [4096, 128], P(('leaf', 'grid')), may hold values from -0.5 to 0.5
- basis_upper: float32 [4096, 256], P(('leaf', 'grid')), may hold values from -0.125 to 0.125
- pivot_upper: float32 [4096], P(('leaf', 'grid')), may hold values from -2 to 2
- couple_upper: float32 [4096, 128], P(('leaf', 'grid')), may hold values from -0.5 to 0.5
- ranks_upper: int32 [2, 2], replicated, may hold values from 32 to 128
- targets_upper: int32 [4096], P(('leaf', 'grid')), may hold values from 0 to 4095, as said below
- source_root: float32 [8, 4096], P(None, ('leaf', 'grid')), may hold values from -6 to 6
- block_root: float32 [4096, 128], P(('leaf', 'grid')), may hold values from -0.5 to 0.5
- expand_root: float32 [4096, 128], P(('leaf', 'grid')), may hold values from -0.5 to 0.5
- basis_root: float32 [4096, 256], P(('leaf', 'grid')), may hold values from -0.09375 to 0.09375
- pivot_root: float32 [4096], P(('leaf', 'grid')), may hold values from -2 to 2
- ranks_root: int32 [1, 2], replicated, may hold values from 32 to 128
Outputs:
- answer_leaf: float32 [8, 4096], P(None, ('leaf', 'grid'))
- answer_middle: float32 [8, 4096], P(None, ('leaf', 'grid'))
- answer_upper: float32 [8, 4096], P(None, ('leaf', 'grid'))
- answer_root: float32 [8, 4096], P(None, ('leaf', 'grid'))
Inputs may be any that keep to these rules, and one draw needn't show every extreme that they name: `targets_leaf`: within one leaf front the 1024 entries are distinct; each names a row of the parent front's row vector of 2048 rows. Split that vector's separator part and its update part each evenly, in order, over the parent's devices (leaf then grid); then the rows of one device name at most 32 rows held by any one of them, and exactly that many for some. `targets_middle`: within one middle front the entries are distinct; each names a row of the parent front's row vector of 4096 rows. Split likewise over the parent's devices, the rows of one device name at most 8 rows held by any one of them, and exactly that many for some. `targets_upper`: within one upper front the entries are distinct; each names a row of the root separator. Split evenly in order over all devices, the rows of one device name at most 4 rows held by any one of them, and exactly that many for some.
All inputs are finite; a program needn't handle non-finite values.
Results may differ from a plain program's by a relative error of at most 0.0003.
Values sent between devices are 32-bit elements; how exact they have to be, the bound alone decides.
A program may use at most 128 MiB of HBM per device.

v0:
```python
import functools

import jax
import jax.numpy as jnp
from jax import lax
from jax.experimental import pallas as pl
from jax.experimental.pallas import tpu as pltpu
from jax.sharding import PartitionSpec as P

RANK = 128
LANES = 128
MESH = pl.DeviceIdType.MESH
F32 = jnp.float32
BF16 = jnp.bfloat16


def once(a, b, ca, cb):
    return lax.dot_general(a, b, (((ca,), (cb,)), ((), ())), preferred_element_type=F32)


def halves(x):
    hi = x.astype(BF16)
    return hi, (x - hi.astype(F32)).astype(BF16)


def dot(a, b, ca, cb):
    ah, al = halves(a)
    bh, bl = halves(b)
    if ca == 0:
        return once(ah, bh, ca, cb) + (once(al, bh, ca, cb) + once(ah, bl, ca, cb))
    n = a.shape[0]
    both = once(jnp.concatenate([ah.astype(F32), al.astype(F32)], axis=0).astype(BF16), bh, ca, cb)
    return both[:n] + (both[n:] + once(ah, bl, ca, cb))


def pieces3(x):
    hi = x.astype(BF16)
    rest = x - hi.astype(F32)
    mid = rest.astype(BF16)
    return hi, mid, (rest - mid.astype(F32)).astype(BF16)


def mult(a, b):
    return dot(a, b, 1, 0)


def outer(a, b):
    return dot(a, b, 1, 1)


def inner(a, b):
    return dot(a, b, 0, 0)


def split3(x):
    hi = x.astype(BF16).astype(F32)
    rest = x - hi
    mid = rest.astype(BF16).astype(F32)
    return jnp.concatenate([hi, mid, rest - mid], axis=0).astype(BF16)


def select(x, onehot, cb):
    out = once(split3(x), onehot, 1, cb)
    n = x.shape[0]
    return out[:n] + out[n : 2 * n] + out[2 * n :]


def kernel(cfg, names, *refs):
    leaves, across, size, ups, count, caps = cfg
    total_devices = leaves * across
    (src, blk, exp, bas, piv, rnk) = [refs[4 * i : 4 * i + 4] for i in range(6)]
    cpl = refs[24:27]
    tgt = refs[27:30]
    outs = refs[30:34]
    m = dict(zip(names, refs[34:-2]))
    send_sem, recv_sem = refs[-2:]
    sems = {}

    me = lax.axis_index("leaf") * across + lax.axis_index("grid")
    plane = size[1]
    planes = total_devices // plane
    spot = me % plane
    layer = me // plane
    late = total_devices > 64
    pending = []

    def where(peer):
        return (peer // across, peer % across)

    def sem_of(name):
        return sems.setdefault(name, len(sems))

    def remote(a, b, sem, peer):
        return pltpu.make_async_remote_copy(
            src_ref=a,
            dst_ref=b,
            send_sem=send_sem.at[sem],
            recv_sem=recv_sem.at[sem],
            device_id=where(peer),
            device_id_type=MESH,
        )

    def wait_for(part, sem):
        pltpu.make_async_copy(part, part, sem).wait()

    def send_each(source, dest, group, name, stride=1):
        idx = me // stride % group
        base = me - idx * stride
        sem = sem_of(name)

        def body(k, carry):
            q = (idx + k) % group
            remote(source(q), dest(idx), sem, base + q * stride).start()
            return carry

        lax.fori_loop(1, group, body, 0)

    def send_all(name, group, stride=1):
        buf = m[name]
        idx = me // stride % group
        send_each(lambda q: buf.at[idx], lambda i: buf.at[i], group, name, stride)
        pending.append((buf.at[pl.ds(0, group - 1)], sem_of(name)))

    def arrive(name, group):
        wait_for(m[name].at[pl.ds(0, group - 1)], recv_sem.at[sem_of(name)])

    barrier = pltpu.get_barrier_semaphore()

    def greet(k, carry):
        pl.semaphore_signal(
            barrier, inc=1, device_id=where((me + k) % total_devices), device_id_type=MESH
        )
        return carry

    lax.fori_loop(1, total_devices, greet, 0)

    col = lax.broadcasted_iota(jnp.int32, (count, RANK), 1)

    def mask(level, front, which):
        return (col < rnk[level][front, which]).astype(F32)

    def local_forward(level, b):
        local = mult(b, blk[level][...])
        bq = mult(b, bas[level][:, :RANK])
        lv = mult(local, bas[level][:, RANK:]) if level < 3 else None
        return local, bq, lv

    parts_of = [min(size[level], 16) for level in range(3)]

    def scatter_cross(level):
        g = size[level]
        p = parts_of[level]
        rp = RANK // p
        idx = me % g
        base = me - idx
        sem = sem_of(("rs", level))
        cross_p, rs_buf = m["cross_p", level], m["rs", level]

        def body(k, carry):
            q = (idx + k) % p

            def go():
                rows = pl.ds(pl.multiple_of(q * rp, 8), rp)
                remote(cross_p.at[rows], rs_buf.at[idx], sem, base + q).start()

            if g == p:
                go()
            else:
                pl.when(q != idx)(go)
            return carry

        lax.fori_loop(1 if g == p else 0, p, body, 0)

        def keep():
            rows = pl.ds(pl.multiple_of(idx * rp, 8), rp)
            rs_buf[idx] = cross_p[rows, :]

        if g == p:
            keep()
        else:
            pl.when(idx < p)(keep)

    def ship_couple(level):
        gp = size[level + 1]
        u = ups[level]
        cap = caps[level]
        wide = max(8, cap)
        sep = gp * LANES
        t = tgt[level][...]
        upd = t >= sep
        rel = jnp.where(upd, t - sep, t)
        dst = rel // LANES
        low = rel % LANES + jnp.where(upd, LANES, 0)
        ri = lax.broadcasted_iota(jnp.int32, (u, u), 0)
        ci = lax.broadcasted_iota(jnp.int32, (u, u), 1)
        dst_f = dst.astype(F32)
        dst_c = jnp.sum(jnp.where(ri == ci, jnp.broadcast_to(dst_f, (u, u)), 0.0), axis=1, keepdims=True)
        rank = jnp.sum(
            jnp.where((dst_c == dst_f) & (ri < ci), 1.0, 0.0), axis=0, keepdims=True
        ).astype(jnp.int32)
        pos = dst * wide + rank
        slots = gp * wide
        si = lax.broadcasted_iota(jnp.int32, (slots, u), 0)
        hit = (si == pos).astype(F32)
        hit16 = hit.astype(BF16)
        hi, mid, lo = [once(hit16, piece, 1, 0) for piece in pieces3(cpl[level][...])]
        moved = hi + mid + lo
        perm_buf, recv_c = m["perm", level], m["couple", level]
        if cap <= 4:
            shifted = (si == pos + 4).astype(F32)
            lowc = jnp.sum(shifted * low.astype(F32), axis=1, keepdims=True)
            both = moved + jnp.broadcast_to(lowc, (slots, LANES))
        else:
            lowc = jnp.sum(hit * low.astype(F32), axis=1, keepdims=True)
            both = jnp.concatenate([moved, jnp.broadcast_to(lowc, (slots, LANES))], axis=1)
        perm_buf[...] = both.reshape(gp, wide, both.shape[1])
        idx = me % gp
        recv_c[idx] = perm_buf[idx]
        send_each(lambda q: perm_buf.at[q], lambda i: recv_c.at[i], gp, ("couple", level))
        pending.append((perm_buf.at[pl.ds(0, gp - 1)], sem_of(("couple", level))))

    def gather_cross(level):
        g = size[level]
        gp = size[level + 1]
        p = parts_of[level]
        idx = me % g
        place = me % gp
        sem = sem_of(("cross", level))
        slot = place // g * p + idx
        buf, rs_buf = m["cross", level], m["rs", level]

        def go():
            wait_for(rs_buf.at[pl.ds(0, g - 1)], recv_sem.at[sem_of(("rs", level))])
            buf[slot] = jnp.sum(rs_buf[...], axis=0)

            def body(k, carry):
                peer = me - place + (place + k) % gp
                remote(buf.at[slot], buf.at[slot], sem, peer).start()
                return carry

            lax.fori_loop(1, gp, body, 0)

        if g == p:
            go()
        else:
            pl.when(idx < p)(go)

    def build_gt(level):
        g = size[level]
        gp = size[level + 1]
        wide = max(8, caps[level])
        nch = gp // g
        gt = m["gt", level]
        rows = gt.shape[1]
        arrive(("couple", level), gp)
        slots = g * wide
        lane = lax.broadcasted_iota(jnp.int32, (slots, rows), 1).astype(F32)
        for child in range(nch):
            got = m["couple", level][child * g : (child + 1) * g]
            got = got.reshape(slots, got.shape[2])
            if caps[level] <= 4:
                up = jnp.concatenate([got[4:, :1], got[:4, :1]], axis=0)
                si = lax.broadcasted_iota(jnp.int32, (slots, 1), 0)
                low = jnp.where(si % 8 < 4, up, -1.0)
            else:
                low = got[:, LANES : LANES + 1]
            ot = (lane == low).astype(F32).astype(BF16)
            hi, mid, lo = [once(piece, ot, 0, 0) for piece in pieces3(got[:, :LANES])]
            gt[child * RANK : (child + 1) * RANK, :] = hi + mid + lo

    def arrive_cross(level):
        g = size[level]
        p = parts_of[level]
        n = size[level + 1] // g * p
        sem = recv_sem.at[sem_of(("cross", level))]
        buf = m["cross", level]
        if g == p:
            wait_for(buf.at[pl.ds(0, n - 1)], sem)
        else:
            idx = me % g
            pl.when(idx < p)(lambda: wait_for(buf.at[pl.ds(0, n - 1)], sem))
            pl.when(idx >= p)(lambda: wait_for(buf.at[pl.ds(0, n)], sem))

    def cross_of(level, child):
        p = parts_of[level]
        return m["cross", level][pl.ds(child * p, p)].reshape(RANK, RANK)

    def build_bot_middle():
        gp = size[2]
        place = me % gp
        rows = 2 * LANES
        ri = lax.broadcasted_iota(jnp.int32, (rows, LANES), 0)
        arrive("tgt_middle", gp)
        mine = jnp.where(ri < LANES, place * LANES + ri, (gp + place - 1) * LANES + ri).astype(F32)

        def fill(j, carry):
            t = m["tgt_middle"][j][0:1, :]
            lanes = pl.ds(pl.multiple_of(j * LANES, LANES), LANES)
            m["bot_middle"][:, lanes] = (mine == t).astype(F32).astype(BF16)
            return carry

        lax.fori_loop(0, gp, fill, 0)

    def build_bot_upper():
        rows = planes * LANES
        ri = lax.broadcasted_iota(jnp.int32, (rows, LANES), 0)
        arrive("tgt_upper", plane)
        mine = ((ri // LANES * plane + spot) * LANES + ri % LANES).astype(F32)

        def fill(j, carry):
            t = m["tgt_upper"][j][0:1, :]
            lanes = pl.ds(pl.multiple_of(j * LANES, LANES), LANES)
            m["bot_upper"][:, lanes] = (mine == t).astype(F32).astype(BF16)
            return carry

        lax.fori_loop(0, plane, fill, 0)

    def build_ft_middle():
        t = tgt[1][...]
        ri = lax.broadcasted_iota(jnp.int32, (LANES, LANES), 0)

        def fill(j, carry):
            rows = pl.ds(pl.multiple_of(j * LANES, LANES), LANES)
            m["ft_middle"][rows, :] = (ri + j * LANES == t).astype(F32).astype(BF16)
            return carry

        lax.fori_loop(0, m["ft_middle"].shape[0] // LANES, fill, 0)

    def build_ft_upper():
        arrive("tgt_layer", planes)
        t = jnp.concatenate([m["tgt_layer"][j][0:1, :] for j in range(planes)], axis=1)
        ri = lax.broadcasted_iota(jnp.int32, (LANES, planes * LANES), 0)

        def fill(j, carry):
            rows = pl.ds(pl.multiple_of(j * LANES, LANES), LANES)
            here = ((ri + (layer * plane + j) * LANES).astype(F32) == t).astype(F32)
            m["ft_upper"][rows, :] = here.astype(BF16)
            return carry

        lax.fori_loop(0, plane, fill, 0)

    def total_sum(value, name):
        m[name, "a"][spot] = value
        send_all((name, "a"), plane)
        arrive((name, "a"), plane)
        m[name, "b"][layer] = jnp.sum(m[name, "a"][...], axis=0)
        send_all((name, "b"), planes, plane)

    def total_arrived(name):
        arrive((name, "b"), planes)
        return jnp.sum(m[name, "b"][...], axis=0)

    def share(level, zp):
        m["zp", level][me % size[level]] = zp
        send_all(("zp", level), size[level])

    def shared(level):
        arrive(("zp", level), size[level])
        return jnp.sum(m["zp", level][...], axis=0)

    local, bq, lv = local_forward(0, src[0][...])
    m["f1"][spot] = jnp.concatenate([bq, lv], axis=0)
    m["cross_p", 0][...] = inner(exp[0][...], bas[0][:, RANK:])
    pl.semaphore_wait(barrier, total_devices - 1)
    send_all("f1", plane)
    scatter_cross(0)
    ship_couple(0)
    for level in (1, 2):
        m["cross_p", level][...] = inner(exp[level][...], bas[level][:, RANK:])
        scatter_cross(level)
    m["tgt_middle"][me % size[2]] = jnp.broadcast_to(tgt[1][...], (8, LANES)).astype(F32)
    send_all("tgt_middle", size[2])
    gather_cross(0)
    ship_couple(1)
    gather_cross(1)
    mine_t = jnp.broadcast_to(tgt[2][...], (8, LANES)).astype(F32)
    m["tgt_upper"][spot] = mine_t
    send_all("tgt_upper", plane)
    m["tgt_layer"][layer] = mine_t
    send_all("tgt_layer", planes, plane)
    build_gt(0)

    saved = []
    inc_upd = None
    for level in range(3):
        g = size[level]
        gp = size[level + 1]
        nch = gp // g
        place = me % gp
        parent = me // gp
        child_me = place // g
        arrive_cross(level)
        if level < 2:
            name = ("f1", "f2")[level]
            buf, step = m[name], g
            arrive(name, gp)
        else:
            buf, step = m["f3b"], g // plane
            arrive("f3b", planes)
        ws = []
        for child in range(nch):
            tot = jnp.sum(buf[child * step : (child + 1) * step, : 2 * count, :], axis=0)
            front = parent * nch + child
            hq = tot[:count] * mask(level, front, 0)
            cross = cross_of(level, child)
            ws.append((tot[count:] + mult(hq, cross)) * mask(level, front, 1))
        inc = -mult(jnp.concatenate(ws, axis=1), m["gt", level][...])
        if level == 1:
            rows = jnp.concatenate([buf[j, 2 * count : 3 * count, :] for j in range(gp)], axis=1)
            inc = inc + select(rows, m["bot_middle"][...], 1)
        if level == 2:
            inc = inc + jnp.sum(buf[:, 2 * count : 3 * count, :], axis=0)
        bn = src[level + 1][...] + inc[:, :LANES]
        local_n, bq_n, lv_n = local_forward(level + 1, bn)
        if level == 0:
            m["f2"][me % size[2]] = jnp.concatenate([bq_n, lv_n, inc[:, LANES:]], axis=0)
            send_all("f2", size[2])
        elif level == 1:
            m["f3a"][spot] = jnp.concatenate([bq_n, lv_n, inc[:, LANES:]], axis=0)
            send_all("f3a", plane)
        else:
            m["f4", "a"][spot] = bq_n
            send_all(("f4", "a"), plane)
        own = jnp.sum(buf[pl.ds(child_me * step, step), :count, :], axis=0)
        hq = own * mask(level, me // g, 0)
        z = (local + outer(hq, exp[level][...])) * piv[level][...]
        saved.append(z)
        share(level, mult(z, exp[level][...]))
        if level == 0:
            ship_couple(2)
            gather_cross(2)
            build_gt(1)
            build_bot_middle()
        elif level == 1:
            build_bot_upper()
            arrive("f3a", plane)
            sums = jnp.sum(m["f3a"][:, : 2 * count, :], axis=0)
            rows = jnp.concatenate([m["f3a"][j, 2 * count :, :] for j in range(plane)], axis=1)
            part = select(rows, m["bot_upper"][...], 1)
            for q in range(planes):
                m["f3s"][q] = jnp.concatenate([sums, part[:, q * LANES : (q + 1) * LANES]], axis=0)
            m["f3b"][layer] = m["f3s"][layer]
            send_each(lambda q: m["f3s"].at[q], lambda i: m["f3b"].at[i], planes, "f3b", plane)
            pending.append((m["f3s"].at[pl.ds(0, planes - 1)], sem_of("f3b")))
            build_gt(2)
        else:
            arrive(("f4", "a"), plane)
            m["f4", "b"][layer] = jnp.sum(m["f4", "a"][...], axis=0)
            send_all(("f4", "b"), planes, plane)
        local = local_n

    build_ft_upper()
    hq = total_arrived("f4") * mask(3, 0, 0)
    z = (local + outer(hq, exp[3][...])) * piv[3][...]
    total_sum(mult(z, exp[3][...]), "f5")
    if not late:
        build_ft_middle()
    x = outer(z, blk[3][...])
    rp_total = total_arrived("f5") * mask(3, 0, 0)
    x = x + outer(rp_total, bas[3][:, :RANK])

    xu = None
    for level in (2, 1, 0):
        g = size[level]
        gp = size[level + 1]
        nch = gp // g
        place = me % gp
        child_me = place // g
        full = x if xu is None else jnp.concatenate([x, xu], axis=1)
        sp = outer(full, m["gt", level][...])
        pieces = [sp[:, c * RANK : (c + 1) * RANK] for c in range(nch)]
        if level == 2:
            m["b1a"][spot] = jnp.concatenate(pieces + [x], axis=0)
            send_all("b1a", plane)
            outs[3][...] = x
            arrive("b1a", plane)
            o = nch * count
            sums = jnp.sum(m["b1a"][:, :o, :], axis=0)
            rows = jnp.concatenate([m["b1a"][j, o:, :] for j in range(plane)], axis=1)
            part = select(rows, m["ft_upper"][...], 0)
            for q in range(planes):
                c = q * plane // g
                m["b1s"][q] = jnp.concatenate(
                    [sums[c * count : (c + 1) * count], part[:, q * LANES : (q + 1) * LANES]], axis=0
                )
            m["b1b"][layer] = m["b1s"][layer]
            send_each(lambda q: m["b1s"].at[q], lambda i: m["b1b"].at[i], planes, "b1b", plane)
            pending.append((m["b1s"].at[pl.ds(0, planes - 1)], sem_of("b1b")))
            arrive("b1b", planes)
            both = jnp.sum(m["b1b"][...], axis=0)
            s, xu = both[:count], both[count:]
        else:
            name = ("b3", "b2")[level]
            buf, piece = m[name], m["piece", level]
            for c in range(nch):
                piece[c] = pieces[c]
            head = pl.ds(0, count)
            rest = pl.ds(count, 2 * count)
            buf[place, head] = piece[child_me]
            if level == 1:
                buf[place, rest] = jnp.concatenate([x, xu], axis=0)

                def ship(k, carry, gp=gp, g=g, place=place, buf=buf, piece=piece, name=name):
                    q = (place + k) % gp
                    peer = me - place + q
                    sem = sem_of(name)
                    remote(piece.at[q // g], buf.at[place, head], sem, peer).start()
                    remote(buf.at[place, rest], buf.at[place, rest], sem, peer).start()
                    return carry

                lax.fori_loop(1, gp, ship, 0)
            else:
                send_each(lambda q: piece.at[q // g], lambda i: buf.at[i], gp, name)
            pending.append((buf.at[pl.ds(0, gp - 1)], sem_of(name)))
            outs[level + 1][...] = x
            arrive(name, gp)
            s = jnp.sum(buf[:, head, :], axis=0)
            if level == 1:
                blocks = [buf[j, count : 2 * count, :] for j in range(gp)]
                blocks += [buf[j, 2 * count :, :] for j in range(gp)]
                if late:
                    build_ft_middle()
                xu = select(jnp.concatenate(blocks, axis=1), m["ft_middle"][...], 0)
        s = s * mask(level, me // g, 1)
        r = saved[level] - outer(s, bas[level][:, RANK:])
        proj = (shared(level) - outer(s, cross_of(level, child_me))) * mask(level, me // g, 0)
        x = outer(r, blk[level][...]) + outer(proj, bas[level][:, :RANK])
    outs[0][...] = x

    for part, sem in pending:
        wait_for(part, send_sem.at[sem])
    for level in range(3):
        g = size[level]
        p = parts_of[level]
        rp = RANK // p
        n = size[level + 1] // g * p
        idx = me % g
        rs_sem = send_sem.at[sem_of(("rs", level))]
        ag_sem = send_sem.at[sem_of(("cross", level))]
        cross_p, buf = m["cross_p", level], m["cross", level]

        def ag_done():
            for _ in range(g // p - 1):
                wait_for(buf.at[pl.ds(0, n)], ag_sem)
            wait_for(buf.at[pl.ds(0, n - 1)], ag_sem)

        if g == p:
            wait_for(cross_p.at[pl.ds(0, (p - 1) * rp)], rs_sem)
            ag_done()
        else:
            pl.when(idx < p)(lambda: wait_for(cross_p.at[pl.ds(0, (p - 1) * rp)], rs_sem))
            pl.when(idx >= p)(lambda: wait_for(cross_p, rs_sem))
            pl.when(idx < p)(ag_done)


def solution(mesh):
    leaves, across = mesh.shape["leaf"], mesh.shape["grid"]

    def shards(*args):
        levels = [args[8 * i : 8 * i + 8] for i in range(3)]
        root = args[24:30]
        (sl, bl, el, qs, pv, cl, rk, tg) = zip(*levels)
        src = list(sl) + [root[0]]
        blk = list(bl) + [root[1]]
        exp = list(el) + [root[2]]
        bas = list(qs) + [root[3]]
        piv = [v.reshape(1, -1) for v in list(pv) + [root[4]]]
        rnk = list(rk) + [root[5]]
        tgt = [t.reshape(1, -1) for t in tg]
        count = src[0].shape[0]
        ups = [t.shape[1] for t in tgt]
        fronts = [r.shape[0] for r in rnk]
        size = [leaves * across // f for f in fronts]
        for v in src:
            assert v.shape[1] == LANES
        vm = lambda *s: pltpu.VMEM(s, F32)
        bits = lambda *s: pltpu.VMEM(s, BF16)
        total = leaves * across
        plane = size[1]
        planes = total // plane
        nch = [size[i + 1] // size[i] for i in range(3)]
        caps = [max(1, -(-ups[i] // size[i + 1])) for i in range(3)]
        parts = [min(size[i], 16) for i in range(3)]
        ft = (size[2] * 2 * LANES, LANES)
        bufs = {
            "f1": vm(plane, 2 * count, LANES),
            "f2": vm(size[2], 3 * count, LANES),
            "f3a": vm(plane, 3 * count, LANES),
            "f3s": vm(planes, 3 * count, LANES),
            "f3b": vm(planes, 3 * count, LANES),
            "b1a": vm(plane, (nch[2] + 1) * count, LANES),
            "b1s": vm(planes, 2 * count, LANES),
            "b1b": vm(planes, 2 * count, LANES),
            "b2": vm(size[2], 3 * count, LANES),
            "b3": vm(size[1], count, LANES),
            "tgt_middle": vm(size[2], 8, LANES),
            "tgt_upper": vm(plane, 8, LANES),
            "tgt_layer": vm(planes, 8, LANES),
            "bot_middle": bits(2 * LANES, size[2] * LANES),
            "bot_upper": bits(planes * LANES, plane * LANES),
            "ft_middle": bits(*ft),
            "ft_upper": bits(plane * LANES, planes * LANES),
        }
        for name in ("f4", "f5"):
            bufs[name, "a"] = vm(plane, count, LANES)
            bufs[name, "b"] = vm(planes, count, LANES)
        for i in range(3):
            wide = LANES if caps[i] <= 4 else 2 * LANES
            bufs["perm", i] = vm(size[i + 1], max(8, caps[i]), wide)
            bufs["couple", i] = vm(size[i + 1], max(8, caps[i]), wide)
            bufs["cross_p", i] = vm(RANK, RANK)
            bufs["rs", i] = vm(size[i], RANK // parts[i], RANK)
            bufs["cross", i] = vm(nch[i] * parts[i], RANK // parts[i], RANK)
            bufs["gt", i] = vm(nch[i] * RANK, LANES * (1 if i == 2 else 2))
            bufs["zp", i] = vm(size[i], count, LANES)
            bufs["piece", i] = vm(nch[i], count, LANES)
        scratch = list(bufs.values())
        scratch += [pltpu.SemaphoreType.DMA((40,)), pltpu.SemaphoreType.DMA((40,))]
        vspec = pl.BlockSpec(memory_space=pltpu.VMEM)
        sspec = pl.BlockSpec(memory_space=pltpu.SMEM)
        return pl.pallas_call(
            functools.partial(kernel, (leaves, across, size, ups, count, caps), list(bufs)),
            out_shape=[jax.ShapeDtypeStruct(v.shape, F32) for v in src],
            in_specs=[vspec] * 20 + [sspec] * 4 + [vspec] * 6,
            out_specs=[vspec] * 4,
            scratch_shapes=scratch,
            compiler_params=pltpu.CompilerParams(
                collective_id=0, has_side_effects=True, vmem_limit_bytes=60 * 1024 * 1024
            ),
        )(*src, *blk, *exp, *bas, *piv, *rnk, *cl, *tgt)

    spread = ("leaf", "grid")
    level = (P(None, spread), P(spread, None), P(spread, None), P(spread, None), P(spread))
    mid = level + (P(spread, None), P(), P(spread))
    return jax.shard_map(
        shards,
        mesh=mesh,
        in_specs=mid * 3 + level + (P(),),
        out_specs=(P(None, spread),) * 4,
        check_vma=False,
    )
```

profile of v0, /device:TPU:0, one launch (start us, length us, event | category | flops | bytes accessed | tf_op | source)
XLA Modules:
  0.0 72.4 jit_solution(1159341484944557312)
XLA Ops:
  0.6 0.0 copy-start.4
  0.6 0.7 copy-done.4
  1.3 0.0 copy-start.5
  1.3 0.7 copy.35.refs_21_
  2.0 0.0 copy-done.5
  2.0 0.7 copy.34.refs_20_
  2.7 66.4 %shard_map.309 = (f32[8,128]{1,0:T(8,128)}, f32[8,128]{1,0:T(8,128)}, f32[8,128]{1,0:T(8,128)}, f32[8,128]{1,0:T(8,128)}) custom-call(f32[8,128]{1,0:T(8,128)} %refs_0_.1, f32[8,128]{1,0:T(8,128)} %refs_1_.1, f32[8,128]{1,0:T(8,128)} %refs_2_.1, f32[8,128]{1,0:T(8,128)} %refs_3_.1, f32[128,128]{1,0:T(8,128)} %refs_4_.1, f32[128,128]{1,0:T(8,128)} %refs_5_.1, ...), custom_call_target="tpu_custom_call" | custom-call | tf_op jit(solution)/shard_map/pallas_call | solution.py:621
  69.1 0.0 copy-start.3
  69.1 0.7 copy-done.3
  69.8 0.0 copy-start.2
  69.8 0.6 copy.40
  70.4 0.1 copy-done.2
  70.4 0.0 copy-start.1
  70.4 0.6 copy.41
  71.0 0.1 copy-done.1
  71.1 0.0 copy-start
  71.1 0.6 copy.42
  71.7 0.1 copy-done
  71.8 0.6 copy.43
Async XLA Ops:
  0.6 0.7 copy-start.4
  1.3 0.7 copy-start.5
  69.1 0.7 copy-start.3
  69.8 0.7 copy-start.2
  70.4 0.7 copy-start.1
  71.1 0.7 copy-start
where the time goes:
time: 72.7 us; the launch traced here: 72.4 us
  Pallas kernels  66.4 us (91%)
  local copies, waits for them, and re-layouts  5.31 us (7%)
    pallas_call x1, Pallas kernels, shards(): pl.pallas_call(functools.partial(kernel, (leaves, across, size, ups, coun...  66.4 us
    unnamed x18, local copies, waits for them, and re-layouts  5.31 us

commit v1 on v0

--- a/solution.py
+++ b/solution.py
@@ -65,16 +65,22 @@
     return out[:n] + out[n : 2 * n] + out[2 * n :]
 
 
+KINDS = ("src", "blk", "exp", "bas", "piv", "rnk")
+
+
 def kernel(cfg, names, *refs):
-    leaves, across, size, ups, count, caps = cfg
+    leaves, across, size, ups, count, caps, fronts = cfg
     total_devices = leaves * across
-    (src, blk, exp, bas, piv, rnk) = [refs[4 * i : 4 * i + 4] for i in range(6)]
-    cpl = refs[24:27]
-    tgt = refs[27:30]
+    hbm = [refs[4 * i : 4 * i + 4] for i in range(6)]
+    cpl_in = refs[24:27]
+    tgt_in = refs[27:30]
     outs = refs[30:34]
-    m = dict(zip(names, refs[34:-2]))
-    send_sem, recv_sem = refs[-2:]
+    m = dict(zip(names, refs[34:-3]))
+    send_sem, recv_sem, load_sem = refs[-3:]
     sems = {}
+    src, blk, exp, bas, piv, rnk = [[m[k, i] for i in range(4)] for k in KINDS]
+    cpl = [m["cpl", i] for i in range(3)]
+    tgt = [m["tgt", i] for i in range(3)]
 
     me = lax.axis_index("leaf") * across + lax.axis_index("grid")
     plane = size[1]
@@ -83,6 +89,31 @@
     layer = me // plane
     late = total_devices > 64
     pending = []
+
+    loads = {}
+    loaded = set()
+    order = [("src", 0), ("bas", 0), ("blk", 0), ("exp", 0), ("cpl", 0), ("tgt", 0), ("piv", 0)]
+    order += [("rnk", i) for i in range(4)]
+    order += [(k, 1) for k in ("blk", "bas", "exp", "cpl", "tgt", "src", "piv")]
+    order += [(k, 2) for k in ("blk", "bas", "exp", "cpl", "tgt", "src", "piv")]
+    order += [(k, 3) for k in ("blk", "bas", "exp", "src", "piv")]
+    where_from = {(k, i): hbm[j][i] for j, k in enumerate(KINDS) for i in range(4)}
+    for i in range(3):
+        where_from["cpl", i] = cpl_in[i]
+        where_from["tgt", i] = tgt_in[i]
+
+    def load(keys):
+        for key in keys:
+            loads[key] = pltpu.make_async_copy(
+                where_from[key], m[key], load_sem.at[len(loads)]
+            )
+            loads[key].start()
+
+    def need(*keys):
+        for key in keys:
+            if key not in loaded:
+                loaded.add(key)
+                loads[key].wait()
 
     def where(peer):
         return (peer // across, peer % across)
@@ -124,6 +155,7 @@
     def arrive(name, group):
         wait_for(m[name].at[pl.ds(0, group - 1)], recv_sem.at[sem_of(name)])
 
+    load(order[:7])
     barrier = pltpu.get_barrier_semaphore()
 
     def greet(k, carry):
@@ -133,22 +165,71 @@
         return carry
 
     lax.fori_loop(1, total_devices, greet, 0)
-
-    col = lax.broadcasted_iota(jnp.int32, (count, RANK), 1)
-
-    def mask(level, front, which):
-        return (col < rnk[level][front, which]).astype(F32)
+    load(order[7:])
+
+    col = lax.broadcasted_iota(jnp.int32, (count, RANK), 1).astype(F32)
+    mask_slots = {}
+
+    def fill_mask(name, level, front, which):
+        ranks = rnk[level][...].astype(F32)
+        if ranks.shape[0] == 2 and fronts[level] > 2:
+            lane = lax.broadcasted_iota(jnp.int32, ranks.shape, 1)
+            row = lax.broadcasted_iota(jnp.int32, ranks.shape, 0)
+            hit = (lane == front) & (row == which)
+        else:
+            lane = lax.broadcasted_iota(jnp.int32, ranks.shape, 1)
+            row = lax.broadcasted_iota(jnp.int32, ranks.shape, 0)
+            hit = (lane == which) & (row == front)
+        r = jnp.sum(jnp.where(hit, ranks, 0.0), axis=1, keepdims=True)
+        r = jnp.sum(r, axis=0, keepdims=True)
+        slot = mask_slots.setdefault(name, len(mask_slots))
+        m["mask"][slot] = (col < r).astype(F32)
+
+    def mask(*name):
+        return m["mask"][mask_slots[name]]
+
+    def fill_masks(level):
+        need(("rnk", level))
+        fill_mask(("own", level, 0), level, me // size[level], 0)
+        if level == 3:
+            return
+        fill_mask(("own", level, 1), level, me // size[level], 1)
+        nch = size[level + 1] // size[level]
+        for child in range(nch):
+            front = me // size[level + 1] * nch + child
+            fill_mask(("kid", level, child, 1), level, front, 1)
+            if level > 0:
+                fill_mask(("kid", level, child, 0), level, front, 0)
+
+    def build_forward(level):
+        need(("blk", level), ("bas", level), ("piv", level), ("exp", level))
+        if level == 3:
+            pt = exp[3][...].T * piv[3][...]
+            m["cross_p", 3][...] = mult(pt, exp[3][...])
+            last = outer(blk[3][...], pt)
+        else:
+            last = mult(blk[level][...], bas[level][:, RANK:])
+        both = jnp.concatenate([blk[level][...], bas[level][:, :RANK], last], axis=1)
+        hi, lo = halves(both)
+        m["fwd", level, 0][...] = hi
+        m["fwd", level, 1][...] = lo
 
     def local_forward(level, b):
-        local = mult(b, blk[level][...])
-        bq = mult(b, bas[level][:, :RANK])
-        lv = mult(local, bas[level][:, RANK:]) if level < 3 else None
-        return local, bq, lv
-
-    parts_of = [min(size[level], 16) for level in range(3)]
+        need(("src", level))
+        bh, bl = halves(b)
+        wh = m["fwd", level, 0][...]
+        n = b.shape[0]
+        two = once(jnp.concatenate([bh.astype(F32), bl.astype(F32)], axis=0).astype(BF16), wh, 1, 0)
+        out = two[:n] + (two[n:] + once(bh, m["fwd", level, 1][...], 1, 0))
+        return out[:, :RANK], out[:, RANK : 2 * RANK], out[:, 2 * RANK :]
+
+    def group_of(level):
+        return size[level] if level < 3 else plane
+
+    parts_of = [min(group_of(level), 16) for level in range(4)]
 
     def scatter_cross(level):
-        g = size[level]
+        g = group_of(level)
         p = parts_of[level]
         rp = RANK // p
         idx = me % g
@@ -180,11 +261,67 @@
         else:
             pl.when(idx < p)(keep)
 
+    def spread_of(level):
+        return (size[0], size[2], size[3], plane)[level]
+
+    def holds_part(level, go):
+        if group_of(level) == parts_of[level]:
+            go()
+        else:
+            pl.when(me % group_of(level) < parts_of[level])(go)
+
+    def sum_parts(level):
+        g = group_of(level)
+        wait_for(m["rs", level].at[pl.ds(0, g - 1)], recv_sem.at[sem_of(("rs", level))])
+        return jnp.sum(m["rs", level][...], axis=0)
+
+    def cross_planes():
+        buf = m["gram"]
+
+        def go():
+            buf[layer] = sum_parts(3)
+            send_each(lambda q: buf.at[layer], lambda i: buf.at[i], planes, "gram", plane)
+
+        holds_part(3, go)
+
+    def gather_cross(level):
+        g = group_of(level)
+        gp = spread_of(level)
+        p = parts_of[level]
+        idx = me % g
+        place = me % gp
+        sem = sem_of(("cross", level))
+        slot = place // g * p + idx
+        buf = m["cross", level]
+
+        def go():
+            if level == 3:
+                arrive("gram", planes)
+                buf[slot] = jnp.sum(m["gram"][...], axis=0)
+            else:
+                buf[slot] = sum_parts(level)
+
+            def body(k, carry):
+                peer = me - place + (place + k) % gp
+                remote(buf.at[slot], buf.at[slot], sem, peer).start()
+                return carry
+
+            lax.fori_loop(1, gp, body, 0)
+
+        holds_part(level, go)
+
+    def rows_path(level):
+        return caps[level] > 4
+
+    def wide_of(level):
+        return max(8, -(-caps[level] // 8) * 8)
+
     def ship_couple(level):
+        need(("tgt", level), ("cpl", level))
+        g = size[level]
         gp = size[level + 1]
         u = ups[level]
-        cap = caps[level]
-        wide = max(8, cap)
+        wide = wide_of(level)
         sep = gp * LANES
         t = tgt[level][...]
         upd = t >= sep
@@ -195,9 +332,8 @@
         ci = lax.broadcasted_iota(jnp.int32, (u, u), 1)
         dst_f = dst.astype(F32)
         dst_c = jnp.sum(jnp.where(ri == ci, jnp.broadcast_to(dst_f, (u, u)), 0.0), axis=1, keepdims=True)
-        rank = jnp.sum(
-            jnp.where((dst_c == dst_f) & (ri < ci), 1.0, 0.0), axis=0, keepdims=True
-        ).astype(jnp.int32)
+        same = dst_c == dst_f
+        rank = jnp.sum(jnp.where(same & (ri < ci), 1.0, 0.0), axis=0, keepdims=True).astype(jnp.int32)
         pos = dst * wide + rank
         slots = gp * wide
         si = lax.broadcasted_iota(jnp.int32, (slots, u), 0)
@@ -206,72 +342,64 @@
         hi, mid, lo = [once(hit16, piece, 1, 0) for piece in pieces3(cpl[level][...])]
         moved = hi + mid + lo
         perm_buf, recv_c = m["perm", level], m["couple", level]
-        if cap <= 4:
+        idx = me % gp
+        if rows_path(level):
+            rank_c = jnp.sum(jnp.where(same & (ci < ri), 1.0, 0.0), axis=1, keepdims=True)
+            first = (me % g * wide).astype(F32)
+            lane = lax.broadcasted_iota(jnp.int32, (u, LANES), 1).astype(F32)
+            place = (lane == rank_c + first).astype(F32).astype(BF16)
+            qi = lax.broadcasted_iota(jnp.int32, (gp, u), 0)
+            named = jnp.where(qi == dst, low.astype(F32), 0.0).astype(BF16)
+            lows = once(named, place, 1, 0)
+            lows_s, lows_r = m["low_s", level], m["low", level]
+            for q in range(gp):
+                lows_s[q] = lows[q : q + 1, :]
+            lows_r[idx] = lows_s[idx]
+            perm_buf[...] = moved.reshape(gp, wide, LANES)
+        else:
             shifted = (si == pos + 4).astype(F32)
             lowc = jnp.sum(shifted * low.astype(F32), axis=1, keepdims=True)
             both = moved + jnp.broadcast_to(lowc, (slots, LANES))
-        else:
-            lowc = jnp.sum(hit * low.astype(F32), axis=1, keepdims=True)
-            both = jnp.concatenate([moved, jnp.broadcast_to(lowc, (slots, LANES))], axis=1)
-        perm_buf[...] = both.reshape(gp, wide, both.shape[1])
-        idx = me % gp
+            perm_buf[...] = both.reshape(gp, wide, LANES)
         recv_c[idx] = perm_buf[idx]
+        if rows_path(level):
+            send_each(lambda q: lows_s.at[q], lambda i: lows_r.at[i], gp, ("low", level))
+            pending.append((lows_s.at[pl.ds(0, gp - 1)], sem_of(("low", level))))
         send_each(lambda q: perm_buf.at[q], lambda i: recv_c.at[i], gp, ("couple", level))
         pending.append((perm_buf.at[pl.ds(0, gp - 1)], sem_of(("couple", level))))
-
-    def gather_cross(level):
-        g = size[level]
-        gp = size[level + 1]
-        p = parts_of[level]
-        idx = me % g
-        place = me % gp
-        sem = sem_of(("cross", level))
-        slot = place // g * p + idx
-        buf, rs_buf = m["cross", level], m["rs", level]
-
-        def go():
-            wait_for(rs_buf.at[pl.ds(0, g - 1)], recv_sem.at[sem_of(("rs", level))])
-            buf[slot] = jnp.sum(rs_buf[...], axis=0)
-
-            def body(k, carry):
-                peer = me - place + (place + k) % gp
-                remote(buf.at[slot], buf.at[slot], sem, peer).start()
-                return carry
-
-            lax.fori_loop(1, gp, body, 0)
-
-        if g == p:
-            go()
-        else:
-            pl.when(idx < p)(go)
 
     def build_gt(level):
         g = size[level]
         gp = size[level + 1]
-        wide = max(8, caps[level])
+        wide = wide_of(level)
         nch = gp // g
         gt = m["gt", level]
         rows = gt.shape[1]
+        if rows_path(level):
+            arrive(("low", level), gp)
         arrive(("couple", level), gp)
         slots = g * wide
-        lane = lax.broadcasted_iota(jnp.int32, (slots, rows), 1).astype(F32)
         for child in range(nch):
             got = m["couple", level][child * g : (child + 1) * g]
-            got = got.reshape(slots, got.shape[2])
-            if caps[level] <= 4:
+            got = got.reshape(slots, LANES)
+            if rows_path(level):
+                low = jnp.sum(m["low", level][child * g : (child + 1) * g], axis=0)[:, :slots]
+                ri = lax.broadcasted_iota(jnp.int32, (rows, slots), 0).astype(F32)
+                ot = (ri == low).astype(F32).astype(BF16)
+                hi, mid, lo = [once(piece, ot, 0, 1) for piece in pieces3(got)]
+            else:
+                lane = lax.broadcasted_iota(jnp.int32, (slots, rows), 1).astype(F32)
                 up = jnp.concatenate([got[4:, :1], got[:4, :1]], axis=0)
                 si = lax.broadcasted_iota(jnp.int32, (slots, 1), 0)
                 low = jnp.where(si % 8 < 4, up, -1.0)
-            else:
-                low = got[:, LANES : LANES + 1]
-            ot = (lane == low).astype(F32).astype(BF16)
-            hi, mid, lo = [once(piece, ot, 0, 0) for piece in pieces3(got[:, :LANES])]
+                ot = (lane == low).astype(F32).astype(BF16)
+                hi, mid, lo = [once(piece, ot, 0, 0) for piece in pieces3(got)]
             gt[child * RANK : (child + 1) * RANK, :] = hi + mid + lo
 
     def arrive_cross(level):
-        g = size[level]
+        g = group_of(level)
         p = parts_of[level]
-        n = size[level + 1] // g * p
+        n = spread_of(level) // g * p
         sem = recv_sem.at[sem_of(("cross", level))]
         buf = m["cross", level]
         if g == p:
@@ -294,7 +422,7 @@
         mine = jnp.where(ri < LANES, place * LANES + ri, (gp + place - 1) * LANES + ri).astype(F32)
 
         def fill(j, carry):
-            t = m["tgt_middle"][j][0:1, :]
+            t = m["tgt_middle"][j]
             lanes = pl.ds(pl.multiple_of(j * LANES, LANES), LANES)
             m["bot_middle"][:, lanes] = (mine == t).astype(F32).astype(BF16)
             return carry
@@ -308,7 +436,7 @@
         mine = ((ri // LANES * plane + spot) * LANES + ri % LANES).astype(F32)
 
         def fill(j, carry):
-            t = m["tgt_upper"][j][0:1, :]
+            t = m["tgt_upper"][j]
             lanes = pl.ds(pl.multiple_of(j * LANES, LANES), LANES)
             m["bot_upper"][:, lanes] = (mine == t).astype(F32).astype(BF16)
             return carry
@@ -328,7 +456,7 @@
 
     def build_ft_upper():
         arrive("tgt_layer", planes)
-        t = jnp.concatenate([m["tgt_layer"][j][0:1, :] for j in range(planes)], axis=1)
+        t = jnp.concatenate([m["tgt_layer"][j] for j in range(planes)], axis=1)
         ri = lax.broadcasted_iota(jnp.int32, (LANES, planes * LANES), 0)
 
         def fill(j, carry):
@@ -339,17 +467,6 @@
 
         lax.fori_loop(0, plane, fill, 0)
 
-    def total_sum(value, name):
-        m[name, "a"][spot] = value
-        send_all((name, "a"), plane)
-        arrive((name, "a"), plane)
-        m[name, "b"][layer] = jnp.sum(m[name, "a"][...], axis=0)
-        send_all((name, "b"), planes, plane)
-
-    def total_arrived(name):
-        arrive((name, "b"), planes)
-        return jnp.sum(m[name, "b"][...], axis=0)
-
     def share(level, zp):
         m["zp", level][me % size[level]] = zp
         send_all(("zp", level), size[level])
@@ -358,29 +475,40 @@
         arrive(("zp", level), size[level])
         return jnp.sum(m["zp", level][...], axis=0)
 
-    local, bq, lv = local_forward(0, src[0][...])
-    m["f1"][spot] = jnp.concatenate([bq, lv], axis=0)
-    m["cross_p", 0][...] = inner(exp[0][...], bas[0][:, RANK:])
-    pl.semaphore_wait(barrier, total_devices - 1)
-    send_all("f1", plane)
-    scatter_cross(0)
-    ship_couple(0)
-    for level in (1, 2):
+    def start_cross(level):
+        need(("exp", level), ("bas", level))
         m["cross_p", level][...] = inner(exp[level][...], bas[level][:, RANK:])
         scatter_cross(level)
-    m["tgt_middle"][me % size[2]] = jnp.broadcast_to(tgt[1][...], (8, LANES)).astype(F32)
+
+    need(("src", 0), ("bas", 0))
+    m["f0"][me % size[0]] = mult(src[0][...], bas[0][:, :RANK])
+    pl.semaphore_wait(barrier, total_devices - 1)
+    send_all("f0", size[0])
+    need(("blk", 0), ("exp", 0), ("piv", 0))
+    ship_couple(0)
+    local = mult(src[0][...], blk[0][...])
+    fill_masks(0)
+    arrive("f0", size[0])
+    hq = jnp.sum(m["f0"][...], axis=0) * mask("own", 0, 0)
+    y = local + outer(hq, exp[0][...])
+    m["f1"][spot] = mult(y, bas[0][:, RANK:])
+    send_all("f1", plane)
+    need(("tgt", 1), ("tgt", 2))
+    m["tgt_middle"][me % size[2]] = tgt[1][...].astype(F32)
     send_all("tgt_middle", size[2])
-    gather_cross(0)
-    ship_couple(1)
-    gather_cross(1)
-    mine_t = jnp.broadcast_to(tgt[2][...], (8, LANES)).astype(F32)
+    mine_t = tgt[2][...].astype(F32)
     m["tgt_upper"][spot] = mine_t
     send_all("tgt_upper", plane)
     m["tgt_layer"][layer] = mine_t
     send_all("tgt_layer", planes, plane)
+    saved = [y * piv[0][...]]
+    start_cross(1)
+    ship_couple(1)
+    build_forward(1)
+    fill_masks(1)
     build_gt(0)
-
-    saved = []
+    start_cross(2)
+
     inc_upd = None
     for level in range(3):
         g = size[level]
@@ -389,7 +517,8 @@
         place = me % gp
         parent = me // gp
         child_me = place // g
-        arrive_cross(level)
+        if level > 0:
+            arrive_cross(level)
         if level < 2:
             name = ("f1", "f2")[level]
             buf, step = m[name], g
@@ -399,17 +528,21 @@
             arrive("f3b", planes)
         ws = []
         for child in range(nch):
-            tot = jnp.sum(buf[child * step : (child + 1) * step, : 2 * count, :], axis=0)
-            front = parent * nch + child
-            hq = tot[:count] * mask(level, front, 0)
-            cross = cross_of(level, child)
-            ws.append((tot[count:] + mult(hq, cross)) * mask(level, front, 1))
+            if level == 0:
+                tot = jnp.sum(buf[child * step : (child + 1) * step], axis=0)
+                ws.append(tot * mask("kid", 0, child, 1))
+            else:
+                tot = jnp.sum(buf[child * step : (child + 1) * step, : 2 * count, :], axis=0)
+                hq = tot[:count] * mask("kid", level, child, 0)
+                cross = cross_of(level, child)
+                ws.append((tot[count:] + mult(hq, cross)) * mask("kid", level, child, 1))
         inc = -mult(jnp.concatenate(ws, axis=1), m["gt", level][...])
         if level == 1:
             rows = jnp.concatenate([buf[j, 2 * count : 3 * count, :] for j in range(gp)], axis=1)
             inc = inc + select(rows, m["bot_middle"][...], 1)
         if level == 2:
             inc = inc + jnp.sum(buf[:, 2 * count : 3 * count, :], axis=0)
+        need(("src", level + 1))
         bn = src[level + 1][...] + inc[:, :LANES]
         local_n, bq_n, lv_n = local_forward(level + 1, bn)
         if level == 0:
@@ -419,20 +552,26 @@
             m["f3a"][spot] = jnp.concatenate([bq_n, lv_n, inc[:, LANES:]], axis=0)
             send_all("f3a", plane)
         else:
-            m["f4", "a"][spot] = bq_n
+            m["f4", "a"][spot] = jnp.concatenate([bq_n, lv_n], axis=0)
             send_all(("f4", "a"), plane)
-        own = jnp.sum(buf[pl.ds(child_me * step, step), :count, :], axis=0)
-        hq = own * mask(level, me // g, 0)
-        z = (local + outer(hq, exp[level][...])) * piv[level][...]
-        saved.append(z)
-        share(level, mult(z, exp[level][...]))
+        if level > 0:
+            own = jnp.sum(buf[pl.ds(child_me * step, step), :count, :], axis=0)
+            hq = own * mask("own", level, 0)
+            saved.append((local + outer(hq, exp[level][...])) * piv[level][...])
+            share(level, mult(saved[level], exp[level][...]))
         if level == 0:
+            gather_cross(1)
             ship_couple(2)
-            gather_cross(2)
+            build_forward(2)
+            fill_masks(2)
             build_gt(1)
             build_bot_middle()
+            gather_cross(2)
+            build_forward(3)
+            scatter_cross(3)
         elif level == 1:
             build_bot_upper()
+            fill_masks(3)
             arrive("f3a", plane)
             sums = jnp.sum(m["f3a"][:, : 2 * count, :], axis=0)
             rows = jnp.concatenate([m["f3a"][j, 2 * count :, :] for j in range(plane)], axis=1)
@@ -442,22 +581,29 @@
             m["f3b"][layer] = m["f3s"][layer]
             send_each(lambda q: m["f3s"].at[q], lambda i: m["f3b"].at[i], planes, "f3b", plane)
             pending.append((m["f3s"].at[pl.ds(0, planes - 1)], sem_of("f3b")))
+            cross_planes()
             build_gt(2)
-        else:
+            share(0, mult(saved[0], exp[0][...]))
+            start_cross(0)
+        else:
+            gather_cross(3)
+            gather_cross(0)
             arrive(("f4", "a"), plane)
             m["f4", "b"][layer] = jnp.sum(m["f4", "a"][...], axis=0)
             send_all(("f4", "b"), planes, plane)
         local = local_n
 
     build_ft_upper()
-    hq = total_arrived("f4") * mask(3, 0, 0)
-    z = (local + outer(hq, exp[3][...])) * piv[3][...]
-    total_sum(mult(z, exp[3][...]), "f5")
     if not late:
         build_ft_middle()
-    x = outer(z, blk[3][...])
-    rp_total = total_arrived("f5") * mask(3, 0, 0)
-    x = x + outer(rp_total, bas[3][:, :RANK])
+    arrive_cross(3)
+    arrive_cross(0)
+    arrive(("f4", "b"), planes)
+    both = jnp.sum(m["f4", "b"][...], axis=0)
+    hq = both[:count] * mask("own", 3, 0)
+    z = (local + outer(hq, exp[3][...])) * piv[3][...]
+    rp_total = (both[count:] + mult(hq, cross_of(3, 0))) * mask("own", 3, 0)
+    x = outer(z, blk[3][...]) + outer(rp_total, bas[3][:, :RANK])
 
     xu = None
     for level in (2, 1, 0):
@@ -521,28 +667,33 @@
                 if late:
                     build_ft_middle()
                 xu = select(jnp.concatenate(blocks, axis=1), m["ft_middle"][...], 0)
-        s = s * mask(level, me // g, 1)
+        s = s * mask("own", level, 1)
         r = saved[level] - outer(s, bas[level][:, RANK:])
-        proj = (shared(level) - outer(s, cross_of(level, child_me))) * mask(level, me // g, 0)
+        mine = child_me if level > 0 else 0
+        proj = (shared(level) - outer(s, cross_of(level, mine))) * mask("own", level, 0)
         x = outer(r, blk[level][...]) + outer(proj, bas[level][:, :RANK])
     outs[0][...] = x
 
     for part, sem in pending:
         wait_for(part, send_sem.at[sem])
-    for level in range(3):
-        g = size[level]
+    for level in range(4):
+        g = group_of(level)
         p = parts_of[level]
         rp = RANK // p
-        n = size[level + 1] // g * p
+        gp = spread_of(level)
+        n = gp // g * p
         idx = me % g
         rs_sem = send_sem.at[sem_of(("rs", level))]
         ag_sem = send_sem.at[sem_of(("cross", level))]
         cross_p, buf = m["cross_p", level], m["cross", level]
 
         def ag_done():
-            for _ in range(g // p - 1):
+            for _ in range((gp - 1) // n):
                 wait_for(buf.at[pl.ds(0, n)], ag_sem)
-            wait_for(buf.at[pl.ds(0, n - 1)], ag_sem)
+            if (gp - 1) % n:
+                wait_for(buf.at[pl.ds(0, (gp - 1) % n)], ag_sem)
+            if level == 3:
+                wait_for(m["gram"].at[pl.ds(0, planes - 1)], send_sem.at[sem_of("gram")])
 
         if g == p:
             wait_for(cross_p.at[pl.ds(0, (p - 1) * rp)], rs_sem)
@@ -551,6 +702,16 @@
             pl.when(idx < p)(lambda: wait_for(cross_p.at[pl.ds(0, (p - 1) * rp)], rs_sem))
             pl.when(idx >= p)(lambda: wait_for(cross_p, rs_sem))
             pl.when(idx < p)(ag_done)
+
+
+def put_out(*refs):
+    n = len(refs) // 2
+    ins, outs, sem = refs[:n], refs[n : 2 * n], refs[-1]
+    copies = [pltpu.make_async_copy(ins[i], outs[i], sem.at[i]) for i in range(n)]
+    for c in copies:
+        c.start()
+    for c in copies:
+        c.wait()
 
 
 def solution(mesh):
@@ -570,6 +731,7 @@
         count = src[0].shape[0]
         ups = [t.shape[1] for t in tgt]
         fronts = [r.shape[0] for r in rnk]
+        rnk = [r.T if r.shape[0] > 2 else r for r in rnk]
         size = [leaves * across // f for f in fronts]
         for v in src:
             assert v.shape[1] == LANES
@@ -580,62 +742,85 @@
         planes = total // plane
         nch = [size[i + 1] // size[i] for i in range(3)]
         caps = [max(1, -(-ups[i] // size[i + 1])) for i in range(3)]
-        parts = [min(size[i], 16) for i in range(3)]
+        group = size[:3] + [plane]
+        spread = [size[0], size[2], size[3], plane]
+        parts = [min(g, 16) for g in group]
         ft = (size[2] * 2 * LANES, LANES)
         bufs = {
-            "f1": vm(plane, 2 * count, LANES),
+            "f0": vm(size[0], count, LANES),
+            "f1": vm(plane, count, LANES),
             "f2": vm(size[2], 3 * count, LANES),
             "f3a": vm(plane, 3 * count, LANES),
             "f3s": vm(planes, 3 * count, LANES),
             "f3b": vm(planes, 3 * count, LANES),
+            ("f4", "a"): vm(plane, 2 * count, LANES),
+            ("f4", "b"): vm(planes, 2 * count, LANES),
             "b1a": vm(plane, (nch[2] + 1) * count, LANES),
             "b1s": vm(planes, 2 * count, LANES),
             "b1b": vm(planes, 2 * count, LANES),
             "b2": vm(size[2], 3 * count, LANES),
             "b3": vm(size[1], count, LANES),
-            "tgt_middle": vm(size[2], 8, LANES),
-            "tgt_upper": vm(plane, 8, LANES),
-            "tgt_layer": vm(planes, 8, LANES),
+            "tgt_middle": vm(size[2], 1, LANES),
+            "tgt_upper": vm(plane, 1, LANES),
+            "tgt_layer": vm(planes, 1, LANES),
             "bot_middle": bits(2 * LANES, size[2] * LANES),
             "bot_upper": bits(planes * LANES, plane * LANES),
             "ft_middle": bits(*ft),
             "ft_upper": bits(plane * LANES, planes * LANES),
+            "mask": vm(6 + 2 * sum(nch), count, LANES),
+            "gram": vm(planes, RANK // parts[3], RANK),
         }
-        for name in ("f4", "f5"):
-            bufs[name, "a"] = vm(plane, count, LANES)
-            bufs[name, "b"] = vm(planes, count, LANES)
+        arrays = {"src": src, "blk": blk, "exp": exp, "bas": bas, "piv": piv, "rnk": rnk, "cpl": cl, "tgt": tgt}
+        for name, list_of in arrays.items():
+            for i, v in enumerate(list_of):
+                bufs[name, i] = pltpu.VMEM(v.shape, v.dtype)
+        for i in range(1, 4):
+            bufs["fwd", i, 0] = bits(LANES, 3 * RANK)
+            bufs["fwd", i, 1] = bits(LANES, 3 * RANK)
+        for i in range(4):
+            bufs["cross_p", i] = vm(RANK, RANK)
+            bufs["rs", i] = vm(group[i], RANK // parts[i], RANK)
+            bufs["cross", i] = vm(spread[i] // group[i] * parts[i], RANK // parts[i], RANK)
         for i in range(3):
-            wide = LANES if caps[i] <= 4 else 2 * LANES
-            bufs["perm", i] = vm(size[i + 1], max(8, caps[i]), wide)
-            bufs["couple", i] = vm(size[i + 1], max(8, caps[i]), wide)
-            bufs["cross_p", i] = vm(RANK, RANK)
-            bufs["rs", i] = vm(size[i], RANK // parts[i], RANK)
-            bufs["cross", i] = vm(nch[i] * parts[i], RANK // parts[i], RANK)
+            wide = max(8, -(-caps[i] // 8) * 8)
+            if caps[i] > 4:
+                assert size[i] * wide <= LANES
+                bufs["low_s", i] = vm(size[i + 1], 1, LANES)
+                bufs["low", i] = vm(size[i + 1], 1, LANES)
+            bufs["perm", i] = vm(size[i + 1], wide, LANES)
+            bufs["couple", i] = vm(size[i + 1], wide, LANES)
             bufs["gt", i] = vm(nch[i] * RANK, LANES * (1 if i == 2 else 2))
             bufs["zp", i] = vm(size[i], count, LANES)
             bufs["piece", i] = vm(nch[i], count, LANES)
         scratch = list(bufs.values())
-        scratch += [pltpu.SemaphoreType.DMA((40,)), pltpu.SemaphoreType.DMA((40,))]
+        scratch += [pltpu.SemaphoreType.DMA((40,)) for _ in range(3)]
         vspec = pl.BlockSpec(memory_space=pltpu.VMEM)
-        sspec = pl.BlockSpec(memory_space=pltpu.SMEM)
-        return pl.pallas_call(
-            functools.partial(kernel, (leaves, across, size, ups, count, caps), list(bufs)),
-            out_shape=[jax.ShapeDtypeStruct(v.shape, F32) for v in src],
-            in_specs=[vspec] * 20 + [sspec] * 4 + [vspec] * 6,
+        aspec = pl.BlockSpec(memory_space=pl.ANY)
+        answers = pl.pallas_call(
+            functools.partial(kernel, (leaves, across, size, ups, count, caps, fronts), list(bufs)),
+            out_shape=[pltpu.VMEM(v.shape, F32) for v in src],
+            in_specs=[aspec] * 30,
             out_specs=[vspec] * 4,
             scratch_shapes=scratch,
             compiler_params=pltpu.CompilerParams(
-                collective_id=0, has_side_effects=True, vmem_limit_bytes=60 * 1024 * 1024
+                collective_id=0, has_side_effects=True, vmem_limit_bytes=56 * 1024 * 1024
             ),
         )(*src, *blk, *exp, *bas, *piv, *rnk, *cl, *tgt)
-
-    spread = ("leaf", "grid")
-    level = (P(None, spread), P(spread, None), P(spread, None), P(spread, None), P(spread))
-    mid = level + (P(spread, None), P(), P(spread))
+        return pl.pallas_call(
+            put_out,
+            out_shape=[jax.ShapeDtypeStruct(v.shape, F32) for v in src],
+            in_specs=[vspec] * 4,
+            out_specs=[aspec] * 4,
+            scratch_shapes=[pltpu.SemaphoreType.DMA((4,))],
+        )(*[pltpu.with_memory_space_constraint(v, pltpu.VMEM) for v in answers])
+
+    spread_axes = ("leaf", "grid")
+    level = (P(None, spread_axes), P(spread_axes, None), P(spread_axes, None), P(spread_axes, None), P(spread_axes))
+    mid = level + (P(spread_axes, None), P(), P(spread_axes))
     return jax.shard_map(
         shards,
         mesh=mesh,
         in_specs=mid * 3 + level + (P(),),
-        out_specs=(P(None, spread),) * 4,
+        out_specs=(P(None, spread_axes),) * 4,
         check_vma=False,
     )

time: 72.7 us -> 56.6 us (0.78)
  Pallas kernels: 66.4 us -> 55.7 us
  local copies, waits for them, and re-layouts: 5.31 us -> 0 us
    pallas_call x1, Pallas kernels: 66.4 us -> 55.1 us  [shards(): pl.pallas_call(functools.partial(kernel, (leaves, across, size, ups, coun...]
    unnamed x18 -> x0, local copies, waits for them, and re-layouts: 5.31 us -> none
where the time goes in v1:
time: 56.6 us; the launch traced here: 56.4 us
  Pallas kernels  55.7 us (98%)
  between operations  0.65 us (1%)
    pallas_call x1, Pallas kernels, shards(): pl.pallas_call(functools.partial(kernel, (leaves, across, size, ups, coun...  55.1 us

profile of v1, /device:TPU:0, one launch (start us, length us, event | category | flops | bytes accessed | tf_op | source)
XLA Modules:
  0.0 56.4 jit_solution(17417624006110681652)
XLA Ops:
  0.6 55.1 %shard_map.309 = (f32[8,128]{1,0:T(8,128)S(1)}, f32[8,128]{1,0:T(8,128)S(1)}, f32[8,128]{1,0:T(8,128)S(1)}, f32[8,128]{1,0:T(8,128)S(1)}) custom-call(f32[8,128]{1,0:T(8,128)} %refs_0_.1, f32[8,128]{1,0:T(8,128)} %refs_1_.1, f32[8,128]{1,0:T(8,128)} %refs_2_.1, f32[8,128]{1,0:T(8,128)} %refs_3_.1, f32[128,128]{1,0:T(8,128)} %refs_4_.1, f32[128,128]{1,0:T(8,128)} %refs_5_.1, ...), custom_call_target="tpu_custom_call" | custom-call | tf_op jit(solution)/shard_map/pallas_call | solution.py:799
  55.7 0.6 %shard_map.310 = (f32[8,128]{1,0:T(8,128)}, f32[8,128]{1,0:T(8,128)}, f32[8,128]{1,0:T(8,128)}, f32[8,128]{1,0:T(8,128)}) custom-call(f32[8,128]{1,0:T(8,128)S(1)} %get-tuple-element.8.refs_0_, f32[8,128]{1,0:T(8,128)S(1)} %get-tuple-element.9.refs_1_, f32[8,128]{1,0:T(8,128)S(1)} %get-tuple-element.10.refs_2_, f32[8,128]{1,0:T(8,128)S(1)} %get-tuple-element.11.refs_3_), custom_call_target="tpu_custom_call" | custom-call | tf_op jit(solution)/shard_map/pallas_call | solution.py:809

commit v2 on v1

v2 whole, which is shorter than its diff:
```python
import functools
import math

import jax
import jax.numpy as jnp
from jax import lax
from jax.experimental import pallas as pl
from jax.experimental.pallas import tpu as pltpu
from jax.sharding import PartitionSpec as P

RANK = 128
LANES = 128
MESH = pl.DeviceIdType.MESH
F32 = jnp.float32
BF16 = jnp.bfloat16

(
    N_SRC, N_BLK, N_EXP, N_BAS, N_PIV, N_RNK, N_CPL, N_TGT, N_RULER, N_COUPLE, N_MASK, N_OWN, N_KID,
    N_CROSS_P, N_LAST, N_NEAR, N_FWD, N_GT, N_CROSS, N_RS, N_GRAM, N_PERM, N_HIT, N_LOW_S, N_LOW, N_GTH,
    N_ROWS_S, N_ROWS_R, N_NAMED, N_G_P, N_G_RS, N_G_ZS, N_G_Z, N_G, N_GH, N_Z, N_XZ, N_BACK, N_TGT_MIDDLE,
    N_BOT_MIDDLE, N_TGT_UPPER, N_BOT_UPPER, N_FT_MIDDLE, N_TGT_LAYER, N_FT_UPPER, N_ZP, N_F0, N_F1, N_F2,
    N_F3B, N_F3A, N_F4A, N_HQ, N_F3S, N_F4S, N_F4B, N_B3, N_B2, N_PIECE,
) = range(59)


def once(a, b, ca, cb):
    return lax.dot_general(a, b, (((ca,), (cb,)), ((), ())), preferred_element_type=F32)


def halves(x):
    hi = x.astype(BF16)
    return hi, (x - hi.astype(F32)).astype(BF16)


def dot(a, b, ca, cb):
    ah, al = halves(a)
    bh, bl = halves(b)
    if ca == 0:
        return once(ah, bh, ca, cb) + (once(al, bh, ca, cb) + once(ah, bl, ca, cb))
    n = a.shape[0]
    both = once(jnp.concatenate([ah.astype(F32), al.astype(F32)], axis=0).astype(BF16), bh, ca, cb)
    return both[:n] + (both[n:] + once(ah, bl, ca, cb))


def mult(a, b):
    return dot(a, b, 1, 0)


def outer(a, b):
    return dot(a, b, 1, 1)


def inner(a, b):
    return dot(a, b, 0, 0)


def select(x, onehot, cb):
    hi = x.astype(BF16).astype(F32)
    out = once(jnp.concatenate([hi, x - hi], axis=0).astype(BF16), onehot, 1, cb)
    n = x.shape[0]
    return out[:n] + out[n:]


KINDS = (N_SRC, N_BLK, N_EXP, N_BAS, N_PIV, N_RNK)


def kernel(cfg, names, *refs):
    leaves, across, size, ups, count, caps, fronts = cfg
    total_devices = leaves * across
    hbm = [refs[4 * i : 4 * i + 4] for i in range(6)]
    cpl_in = refs[24:27]
    tgt_in = refs[27:30]
    outs = refs[30:34]
    m = dict(zip(names, refs[34:-4]))
    send_sem, recv_sem, load_sem, up_sem = refs[-4:]
    sems = {}
    src, blk, exp, bas, piv, rnk = [[m[k, i] for i in range(4)] for k in KINDS]
    cpl = [m[N_CPL, i] for i in range(3)]
    tgt = [m[N_TGT, i] for i in range(3)]

    me = lax.axis_index("leaf") * across + lax.axis_index("grid")
    plane = size[1]
    planes = total_devices // plane
    spot = me % plane
    layer = me // plane
    late = total_devices > 64
    pending = []

    shared_sends = total_devices <= 64
    sent_rows = []
    loaded = set()
    order = [[(N_SRC, 0), (N_BAS, 0)], [(N_EXP, 1), (N_BAS, 1)]]
    order += [[(N_CPL, 0), (N_TGT, 0)], [(N_BLK, 0), (N_EXP, 0), (N_PIV, 0)]]
    order += [[(N_RNK, i)] for i in range(4)]
    order += [[(N_BLK, 1), (N_SRC, 1), (N_PIV, 1), (N_CPL, 1), (N_TGT, 1), (N_TGT, 2), (N_CPL, 2)]]
    order += [[(k, i) for k in (N_EXP, N_BAS, N_BLK, N_SRC, N_PIV)] for i in (2, 3)]
    where_from = {(k, i): hbm[j][i] for j, k in enumerate(KINDS) for i in range(4)}
    for i in range(3):
        where_from[N_CPL, i] = cpl_in[i]
        where_from[N_TGT, i] = tgt_in[i]

    def load(some):
        for keys in some:
            for key in keys:
                pltpu.make_async_copy(where_from[key], m[key], load_sem.at[order.index(keys)]).start()

    def rows_in(ref):
        return math.prod(ref.shape) // LANES

    def wait_rows(rows, sem):
        wait_for(m[N_RULER].at[pl.ds(0, rows)], sem)

    def need(*wanted):
        for i, keys in enumerate(order):
            if any(key in keys for key in wanted) and i not in loaded:
                loaded.add(i)
                if len(keys) == 1:
                    wait_for(m[keys[0]], load_sem.at[i])
                else:
                    wait_rows(sum(rows_in(m[key]) for key in keys), load_sem.at[i])

    def where(peer):
        return (lax.div(peer, across), lax.rem(peer, across))

    def sem_of(name):
        return sems.setdefault(name, len(sems))

    def remote(a, b, sem, peer):
        return pltpu.make_async_remote_copy(
            src_ref=a,
            dst_ref=b,
            send_sem=send_sem.at[0 if shared_sends else sem],
            recv_sem=recv_sem.at[sem],
            device_id=where(peer),
            device_id_type=MESH,
        )

    def wait_for(part, sem):
        pltpu.make_async_copy(part, part, sem).wait()

    def send_each(source, dest, group, name, stride=1):
        idx = me // stride % group
        base = me - idx * stride
        sem = sem_of(name)

        def body(k, carry):
            q = lax.rem(idx + k, group)
            remote(source(q), dest(idx), sem, base + q * stride).start()
            return carry

        lax.fori_loop(1, group, body, 0)

    def send_all(name, group, stride=1):
        buf = m[name]
        idx = me // stride % group
        send_each(lambda q: buf.at[idx], lambda i: buf.at[i], group, name, stride)
        pending.append((buf.at[pl.ds(0, group - 1)], sem_of(name)))

    def arrive(name, group):
        wait_for(m[name].at[pl.ds(0, group - 1)], recv_sem.at[sem_of(name)])

    load(order[:3])
    m[N_COUPLE, 2][...] = jnp.zeros(m[N_COUPLE, 2].shape, F32)
    barrier = pltpu.get_barrier_semaphore()

    def greet_near(k, carry):
        peer = me - spot + lax.rem(spot + k, plane)
        pl.semaphore_signal(barrier, inc=1, device_id=where(peer), device_id_type=MESH)
        return carry

    def greet_far(peer, carry):
        pl.semaphore_signal(barrier, inc=1, device_id=where(peer), device_id_type=MESH)
        return carry

    def greet_back(k, carry):
        pl.semaphore_signal(up_sem, inc=1, device_id=where(k * plane + spot), device_id_type=MESH)
        return carry

    lax.fori_loop(1, plane, greet_near, 0)
    lax.fori_loop((layer + 1) * plane, total_devices, greet_far, 0)
    load(order[3:])

    col = lax.broadcasted_iota(jnp.int32, (count, RANK), 1).astype(F32)
    mask_slots = {}

    def fill_mask(name, level, front, which):
        ranks = rnk[level][...].astype(F32)
        if ranks.shape[0] == 2 and fronts[level] > 2:
            lane = lax.broadcasted_iota(jnp.int32, ranks.shape, 1)
            row = lax.broadcasted_iota(jnp.int32, ranks.shape, 0)
            hit = (lane == front) & (row == which)
        else:
            lane = lax.broadcasted_iota(jnp.int32, ranks.shape, 1)
            row = lax.broadcasted_iota(jnp.int32, ranks.shape, 0)
            hit = (lane == which) & (row == front)
        r = jnp.sum(jnp.where(hit, ranks, 0.0), axis=1, keepdims=True)
        r = jnp.sum(r, axis=0, keepdims=True)
        slot = mask_slots.setdefault(name, len(mask_slots))
        m[N_MASK][slot] = (col < r).astype(F32)

    def mask(*name):
        return m[N_MASK][mask_slots[name]]

    def fill_masks(level):
        need((N_RNK, level))
        fill_mask((N_OWN, level, 0), level, me // size[level], 0)
        if level == 3:
            return
        fill_mask((N_OWN, level, 1), level, me // size[level], 1)
        nch = size[level + 1] // size[level]
        for child in range(nch):
            front = me // size[level + 1] * nch + child
            fill_mask((N_KID, level, child, 1), level, front, 1)

    def build_forward(level):
        need((N_BLK, level), (N_BAS, level), (N_PIV, level), (N_EXP, level))
        parts = [blk[level][...], bas[level][:, :RANK]]
        if level == 3:
            pt = exp[3][...].T * piv[3][...]
            m[N_CROSS_P, 3][...] = mult(pt, exp[3][...])
            m[N_LAST, 3][...] = outer(blk[3][...], pt)
            m[N_NEAR][...] = outer(blk[3][...] * piv[3][...], blk[3][...])
            parts += [m[N_LAST, 3][...], m[N_NEAR][...]]
        else:
            m[N_LAST, level][...] = mult(blk[level][...], bas[level][:, RANK:])
        put_halves((N_FWD, level), 0, jnp.concatenate(parts, axis=1))

    def put_halves(name, start, value, first=0):
        hi, lo = halves(value)
        lanes = slice(start, start + value.shape[1])
        rows = slice(first, first + value.shape[0])
        m[name, 0][rows, lanes] = hi
        m[name, 1][rows, lanes] = lo

    def chain_forward(level):
        top = m[(N_FWD, level), 0][:LANES].astype(F32) + m[(N_FWD, level), 1][:LANES].astype(F32)
        put_halves((N_FWD, level), 0, -mult(m[N_GT, level - 1][:, :LANES], top), LANES)

    def add_cross(level):
        arrive_cross(level)
        heads = bas[level][:, :RANK] * mask(N_OWN, level, 0)[:1]
        yt = m[N_LAST, level][...] + mult(heads, m[N_CROSS, level][...].reshape(RANK, RANK))
        m[N_LAST, level][...] = yt
        if level > 0:
            put_halves((N_FWD, level), 2 * RANK, yt)

    def by_halves(a, name, cb, lanes=slice(None)):
        ah, al = halves(a)
        n = a.shape[0]
        wh = m[name, 0][:, lanes]
        two = once(jnp.concatenate([ah.astype(F32), al.astype(F32)], axis=0).astype(BF16), wh, 1, cb)
        return two[:n] + (two[n:] + once(ah, m[name, 1][:, lanes], 1, cb))

    def local_forward(level, b):
        out = by_halves(b, (N_FWD, level), 0)
        return [out[:, i : i + RANK] for i in range(0, out.shape[1], RANK)]

    def group_of(level):
        return size[level] if level < 3 else plane

    parts_of = [min(group_of(level), 16) for level in range(4)]

    def scatter_cross(level):
        g = group_of(level)
        p = parts_of[level]
        rp = RANK // p
        idx = me % g
        base = me - idx
        sem = sem_of((N_RS, level))
        cross_p, rs_buf = m[N_CROSS_P, level], m[N_RS, level]

        def body(k, carry):
            q = lax.rem(idx + k, p)

            def go():
                rows = pl.ds(pl.multiple_of(q * rp, 8), rp)
                remote(cross_p.at[rows], rs_buf.at[idx], sem, base + q).start()

            if g == p:
                go()
            else:
                pl.when(q != idx)(go)
            return carry

        lax.fori_loop(1 if g == p else 0, p, body, 0)
        sent_rows.append((p - 1) * rp)

        def keep():
            rows = pl.ds(pl.multiple_of(idx * rp, 8), rp)
            rs_buf[idx] = cross_p[rows, :]

        if g == p:
            keep()
        else:
            pl.when(idx < p)(keep)

    def spread_of(level):
        return group_of(level)

    def holds_part(level, go):
        if group_of(level) == parts_of[level]:
            go()
        else:
            pl.when(me % group_of(level) < parts_of[level])(go)

    def sum_parts(level):
        g = group_of(level)
        wait_for(m[N_RS, level].at[pl.ds(0, g - 1)], recv_sem.at[sem_of((N_RS, level))])
        return jnp.sum(m[N_RS, level][...], axis=0)

    def cross_planes():
        buf = m[N_GRAM]

        def go():
            buf[layer] = sum_parts(3)
            send_each(lambda q: buf.at[layer], lambda i: buf.at[i], planes, N_GRAM, plane)
            sent_rows.append((planes - 1) * rows_in(buf) // planes)

        holds_part(3, go)

    def gather_cross(level):
        g = group_of(level)
        gp = spread_of(level)
        p = parts_of[level]
        idx = me % g
        place = me % gp
        sem = sem_of((N_CROSS, level))
        slot = place // g * p + idx
        buf = m[N_CROSS, level]

        def go():
            if level == 3:
                arrive(N_GRAM, planes)
                buf[slot] = jnp.sum(m[N_GRAM][...], axis=0)
            else:
                buf[slot] = sum_parts(level)

            def body(k, carry):
                peer = me - place + lax.rem(place + k, gp)
                remote(buf.at[slot], buf.at[slot], sem, peer).start()
                return carry

            lax.fori_loop(1, gp, body, 0)
            sent_rows.append((gp - 1) * rows_in(buf) // p)

        holds_part(level, go)

    def rows_path(level):
        return size[level] * wide_of(level) <= LANES

    def tucked(level):
        return caps[level] < wide_of(level)

    def couple_rows(level):
        return caps[level] + 1 if rows_path(level) and tucked(level) else wide_of(level)

    def wide_of(level):
        return max(8, -(-caps[level] // 8) * 8)

    def make_couple(level):
        need((N_TGT, level), (N_CPL, level))
        g = size[level]
        gp = size[level + 1]
        u = ups[level]
        wide = wide_of(level)
        sep = gp * LANES
        t = tgt[level][...]
        upd = t >= sep
        rel = jnp.where(upd, t - sep, t)
        dst = rel // LANES
        low = rel % LANES + jnp.where(upd, LANES, 0)
        ri = lax.broadcasted_iota(jnp.int32, (u, u), 0)
        ci = lax.broadcasted_iota(jnp.int32, (u, u), 1)
        dst_f = dst.astype(F32)
        dst_c = jnp.sum(jnp.where(ri == ci, jnp.broadcast_to(dst_f, (u, u)), 0.0), axis=1, keepdims=True)
        same = dst_c == dst_f
        rank = jnp.sum(jnp.where(same & (ri < ci), 1.0, 0.0), axis=0, keepdims=True).astype(jnp.int32)
        pos = dst * wide + rank
        slots = gp * wide
        si = lax.broadcasted_iota(jnp.int32, (slots, u), 0)
        hit = (si == pos).astype(F32)
        hit16 = hit.astype(BF16)
        moved = sum(once(hit16, piece, 1, 0) for piece in halves(cpl[level][...]))
        perm_buf, recv_c = m[N_PERM, level], m[N_COUPLE, level]
        idx = me % gp
        if level == 2:
            m[N_HIT, 0][...] = hit16
            m[N_HIT, 1][...] = (si == pos + 4).astype(F32).astype(BF16)
        if rows_path(level):
            rank_c = jnp.sum(jnp.where(same & (ci < ri), 1.0, 0.0), axis=1, keepdims=True)
            first = (me % g * wide).astype(F32)
            lane = lax.broadcasted_iota(jnp.int32, (u, LANES), 1).astype(F32)
            place = (lane == rank_c + first).astype(F32).astype(BF16)
            low_f = low.astype(F32)
            if tucked(level):
                named = jnp.where(si == dst * wide + caps[level], low_f, 0.0).astype(BF16)
                moved = moved + once(named, place, 1, 0)
            else:
                qi = lax.broadcasted_iota(jnp.int32, (gp, u), 0)
                named = jnp.where(qi == dst, low_f, 0.0).astype(BF16)
                lows = once(named, place, 1, 0)
                lows_s, lows_r = m[N_LOW_S, level], m[N_LOW, level]
                for q in range(gp):
                    lows_s[q] = lows[q : q + 1, :]
                lows_r[idx] = lows_s[idx]
        else:
            shifted = (si == pos + 4).astype(F32)
            lowc = jnp.sum(shifted * low.astype(F32), axis=1, keepdims=True)
            moved = moved + jnp.broadcast_to(lowc, (slots, LANES))
        perm_buf[...] = moved.reshape(gp, wide, LANES)
        recv_c[idx] = perm_buf[idx]

    def send_couple(level):
        gp = size[level + 1]
        perm_buf, recv_c = m[N_PERM, level], m[N_COUPLE, level]
        if rows_path(level) and not tucked(level):
            lows_s, lows_r = m[N_LOW_S, level], m[N_LOW, level]
            send_each(lambda q: lows_s.at[q], lambda i: lows_r.at[i], gp, (N_LOW, level))
            pending.append((lows_s.at[pl.ds(0, gp - 1)], sem_of((N_LOW, level))))
        part = pl.ds(0, couple_rows(level))
        send_each(lambda q: perm_buf.at[q, part], lambda i: recv_c.at[i, part], gp, (N_COUPLE, level))
        pending.append((perm_buf.at[pl.ds(0, gp - 1), part], sem_of((N_COUPLE, level))))

    def ship_couple(level):
        make_couple(level)
        send_couple(level)

    def low_row(level, child):
        g = size[level]
        got = m[N_COUPLE, level] if tucked(level) else m[N_LOW, level]
        one = slice(caps[level], caps[level] + 1) if tucked(level) else slice(0, 1)
        return jnp.sum(got[child * g : (child + 1) * g, one, :], axis=0)[:, : g * wide_of(level)]

    def low_column(level, child):
        g = size[level]
        got = m[N_COUPLE, level][child * g : (child + 1) * g].reshape(g * wide_of(level), LANES)
        si = lax.broadcasted_iota(jnp.int32, (got.shape[0], 1), 0)
        up = jnp.concatenate([got[4:, :1], got[:4, :1]], axis=0)
        return jnp.where(si % 8 < 4, up, -1.0), jnp.where(si % 8 < 4, -1.0, got[:, :1])

    def build_gt(level):
        g = size[level]
        gp = size[level + 1]
        wide = wide_of(level)
        gt = m[N_GT, level]
        rows = gt.shape[1]
        if rows_path(level) and not tucked(level):
            arrive((N_LOW, level), gp)
        got_all = m[N_COUPLE, level]
        wait_for(
            got_all.at[pl.ds(0, gp - 1), pl.ds(0, couple_rows(level))],
            recv_sem.at[sem_of((N_COUPLE, level))],
        )
        slots = g * wide
        for child in range(gp // g):
            got = got_all[child * g : (child + 1) * g].reshape(slots, LANES)
            if rows_path(level):
                if tucked(level):
                    si = lax.broadcasted_iota(jnp.int32, (slots, LANES), 0)
                    got = jnp.where(si % wide < caps[level], got, 0.0)
                ri = lax.broadcasted_iota(jnp.int32, (rows, slots), 0).astype(F32)
                ot = (ri == low_row(level, child)).astype(F32).astype(BF16)
                full = sum(once(piece, ot, 0, 1) for piece in halves(got))
            else:
                lane = lax.broadcasted_iota(jnp.int32, (slots, rows), 1).astype(F32)
                ot = (lane == low_column(level, child)[0]).astype(F32).astype(BF16)
                full = sum(once(piece, ot, 0, 0) for piece in halves(got))
            gt[child * RANK : (child + 1) * RANK, :] = full
            if level < 2:
                put_halves((N_GTH, level), 0, full, child * RANK)

    def reply_rows():
        g = size[2]
        wide = wide_of(2)
        slots = g * wide
        heads = halves(bas[3][:, :RANK])
        tails = halves(m[N_LAST, 3][...])
        for child in range(size[3] // g):
            if rows_path(2):
                low = low_row(2, child)
                lane = lax.broadcasted_iota(jnp.int32, (1, slots), 1) % wide
                one = jnp.where(lane < 4, low, -1.0)
                two = jnp.where(lane < 4, -1.0, pltpu.roll(low, 4, 1))
                iota, by = lax.broadcasted_iota(jnp.int32, (LANES, slots), 0), 0
            else:
                one, two = low_column(2, child)
                iota, by = lax.broadcasted_iota(jnp.int32, (slots, LANES), 1), 1
            iota = iota.astype(F32)
            first = (iota == one).astype(F32).astype(BF16)
            second = (iota == two).astype(F32).astype(BF16)
            rows = once(first, heads[0], by, 0) + once(first, heads[1], by, 0)
            rows = rows + (once(second, tails[0], by, 0) + once(second, tails[1], by, 0))
            m[N_ROWS_S][child * g : (child + 1) * g] = rows.reshape(g, wide, LANES)
        m[N_ROWS_R][me] = m[N_ROWS_S][me]
        send_each(lambda q: m[N_ROWS_S].at[q], lambda i: m[N_ROWS_R].at[i], size[3], N_ROWS_R)
        pending.append((m[N_ROWS_S].at[pl.ds(0, size[3] - 1)], sem_of(N_ROWS_R)))

    def build_named():
        arrive(N_ROWS_R, size[3])
        got = m[N_ROWS_R][...].reshape(size[3] * wide_of(2), LANES)
        pieces = halves(got)
        out = [
            once(pieces[0], m[N_HIT, i][...], 0, 0) + once(pieces[1], m[N_HIT, i][...], 0, 0)
            for i in range(2)
        ]
        put_halves(N_NAMED, 0, jnp.concatenate(out, axis=0))

    g_p = min(plane, 16)
    g_rp = RANK // g_p

    def g_holds(go):
        if plane == g_p:
            go()
        else:
            pl.when(spot < g_p)(go)

    def g_scatter():
        both = jnp.concatenate([bas[3][:, :RANK], m[N_LAST, 3][...]], axis=1)
        full = mult(m[N_GT, 2][...], both)
        n = full.shape[0] // RANK
        for j in range(g_p):
            m[N_G_P][j] = jnp.concatenate(
                [full[c * RANK + j * g_rp : c * RANK + (j + 1) * g_rp] for c in range(n)], axis=0
            )
        sem = sem_of(N_G_RS)

        def body(k, carry):
            q = lax.rem(spot + k, g_p)

            def go():
                remote(m[N_G_P].at[q], m[N_G_RS].at[spot], sem, me - spot + q).start()

            if plane == g_p:
                go()
            else:
                pl.when(q != spot)(go)
            return carry

        lax.fori_loop(1 if plane == g_p else 0, g_p, body, 0)
        sent_rows.append((g_p - 1) * rows_in(m[N_G_P]) // g_p)

        def keep():
            m[N_G_RS][spot] = m[N_G_P][spot]

        g_holds(keep)

    def upper_of(q):
        return q * plane // size[2]

    def g_across():
        def go():
            arrive(N_G_RS, plane)
            total = jnp.sum(m[N_G_RS][...], axis=0)
            for c in range(total.shape[0] // g_rp):
                m[N_G_ZS][c] = total[c * g_rp : (c + 1) * g_rp]
            m[N_G_Z][layer] = m[N_G_ZS][upper_of(layer)]
            send_each(lambda q: m[N_G_ZS].at[upper_of(q)], lambda i: m[N_G_Z].at[i], planes, N_G_Z, plane)
            sent_rows.append((planes - 1) * rows_in(m[N_G_Z]) // planes)

        g_holds(go)

    def g_gather():
        def go():
            arrive(N_G_Z, planes)
            m[N_G][spot] = jnp.sum(m[N_G_Z][...], axis=0)
            send_each(lambda q: m[N_G].at[spot], lambda i: m[N_G].at[i], plane, N_G)
            sent_rows.append((plane - 1) * rows_in(m[N_G]) // g_p)

        g_holds(go)

    def g_arrive():
        sem = recv_sem.at[sem_of(N_G)]
        if plane == g_p:
            wait_for(m[N_G].at[pl.ds(0, g_p - 1)], sem)
        else:
            pl.when(spot < g_p)(lambda: wait_for(m[N_G].at[pl.ds(0, g_p - 1)], sem))
            pl.when(spot >= g_p)(lambda: wait_for(m[N_G].at[pl.ds(0, g_p)], sem))
        hi, lo = halves(m[N_G][...].reshape(RANK, 2 * RANK))
        m[N_GH, 0][...] = hi
        m[N_GH, 1][...] = lo

    def g_drain():
        if plane == g_p:
            wait_for(m[N_G_P].at[pl.ds(0, g_p - 1)], send_sem.at[sem_of(N_G_RS)])
        else:
            pl.when(spot < g_p)(lambda: wait_for(m[N_G_P].at[pl.ds(0, g_p - 1)], send_sem.at[sem_of(N_G_RS)]))
            pl.when(spot >= g_p)(lambda: wait_for(m[N_G_P], send_sem.at[sem_of(N_G_RS)]))

        def go():
            wait_for(m[N_G_Z].at[pl.ds(0, planes - 1)], send_sem.at[sem_of(N_G_Z)])
            n = plane - 1
            while n > 0:
                wait_for(m[N_G].at[pl.ds(0, min(n, g_p))], send_sem.at[sem_of(N_G)])
                n -= g_p

        g_holds(go)

    def prepare_back(level):
        z = m[N_Z, level][...]
        heads = bas[level][:, :RANK]
        own = mask(N_OWN, level, 0)
        xz = outer(z, blk[level][...]) + outer(shared(level) * own, heads)
        yt = m[N_LAST, level][...]
        if level > 0:
            sep = m[N_GT, level - 1][:, :LANES]
            xz = jnp.concatenate([xz, outer(xz, sep)], axis=1)
            yt = jnp.concatenate([yt, mult(sep, yt)], axis=0)
        m[N_XZ, level][...] = xz
        put_halves((N_BACK, level), 0, yt)

    def arrive_cross(level):
        g = group_of(level)
        p = parts_of[level]
        n = spread_of(level) // g * p
        sem = recv_sem.at[sem_of((N_CROSS, level))]
        buf = m[N_CROSS, level]
        if g == p:
            wait_for(buf.at[pl.ds(0, n - 1)], sem)
        else:
            idx = me % g
            pl.when(idx < p)(lambda: wait_for(buf.at[pl.ds(0, n - 1)], sem))
            pl.when(idx >= p)(lambda: wait_for(buf.at[pl.ds(0, n)], sem))

    def build_bot_middle():
        gp = size[2]
        place = me % gp
        rows = 2 * LANES
        ri = lax.broadcasted_iota(jnp.int32, (rows, LANES), 0)
        arrive(N_TGT_MIDDLE, gp)
        mine = jnp.where(ri < LANES, place * LANES + ri, (gp + place - 1) * LANES + ri).astype(F32)

        def fill(j, carry):
            t = m[N_TGT_MIDDLE][j]
            lanes = pl.ds(pl.multiple_of(j * LANES, LANES), LANES)
            m[N_BOT_MIDDLE][:, lanes] = (mine == t).astype(F32).astype(BF16)
            return carry

        lax.fori_loop(0, gp, fill, 0)

    def build_bot_upper():
        rows = planes * LANES
        ri = lax.broadcasted_iota(jnp.int32, (rows, LANES), 0)
        arrive(N_TGT_UPPER, plane)
        mine = ((ri // LANES * plane + spot) * LANES + ri % LANES).astype(F32)

        def fill(j, carry):
            t = m[N_TGT_UPPER][j]
            lanes = pl.ds(pl.multiple_of(j * LANES, LANES), LANES)
            m[N_BOT_UPPER][:, lanes] = (mine == t).astype(F32).astype(BF16)
            return carry

        lax.fori_loop(0, plane, fill, 0)

    def build_ft_middle():
        t = tgt[1][...]
        ri = lax.broadcasted_iota(jnp.int32, (LANES, LANES), 0)

        def fill(j, carry):
            rows = pl.ds(pl.multiple_of(j * LANES, LANES), LANES)
            m[N_FT_MIDDLE][rows, :] = (ri + j * LANES == t).astype(F32).astype(BF16)
            return carry

        lax.fori_loop(0, m[N_FT_MIDDLE].shape[0] // LANES, fill, 0)

    def build_ft_upper():
        arrive(N_TGT_LAYER, planes)
        t = jnp.concatenate([m[N_TGT_LAYER][j] for j in range(planes)], axis=1)
        ri = lax.broadcasted_iota(jnp.int32, (LANES, planes * LANES), 0)

        def fill(j, carry):
            rows = pl.ds(pl.multiple_of(j * LANES, LANES), LANES)
            here = ((ri + (layer * plane + j) * LANES).astype(F32) == t).astype(F32)
            m[N_FT_UPPER][rows, :] = here.astype(BF16)
            return carry

        lax.fori_loop(0, plane, fill, 0)

    def share(level, zp):
        m[N_ZP, level][me % size[level]] = zp
        send_all((N_ZP, level), size[level])

    def shared(level):
        arrive((N_ZP, level), size[level])
        return jnp.sum(m[N_ZP, level][...], axis=0)

    def make_cross(level):
        need((N_EXP, level), (N_BAS, level))
        m[N_CROSS_P, level][...] = inner(exp[level][...], bas[level][:, RANK:])

    def start_cross(level):
        make_cross(level)
        scatter_cross(level)

    need((N_SRC, 0), (N_BAS, 0))
    m[N_F0][me % size[0]] = mult(src[0][...], bas[0][:, :RANK])
    make_cross(1)
    pl.semaphore_wait(barrier, plane - 1 + layer * plane)
    send_all(N_F0, size[0])
    scatter_cross(1)
    lax.fori_loop(0, layer, greet_back, 0)
    ship_couple(0)
    need((N_BLK, 0), (N_EXP, 0), (N_PIV, 0))
    local = mult(src[0][...], blk[0][...])
    fill_masks(0)
    build_forward(1)
    make_cross(2)
    pl.when(layer < planes - 1)(lambda: pl.semaphore_wait(up_sem, planes - 1 - layer))
    scatter_cross(2)
    arrive(N_F0, size[0])
    hq = jnp.sum(m[N_F0][...], axis=0) * mask(N_OWN, 0, 0)
    y = local + outer(hq, exp[0][...])
    m[N_F1][spot] = mult(y, bas[0][:, RANK:])
    send_all(N_F1, plane)
    m[N_Z, 0][...] = y * piv[0][...]
    fill_masks(1)
    gather_cross(1)
    need((N_TGT, 1), (N_TGT, 2))
    m[N_TGT_MIDDLE][me % size[2]] = tgt[1][...].astype(F32)
    send_all(N_TGT_MIDDLE, size[2])
    mine_t = tgt[2][...].astype(F32)
    m[N_TGT_UPPER][spot] = mine_t
    send_all(N_TGT_UPPER, plane)
    m[N_TGT_LAYER][layer] = mine_t
    send_all(N_TGT_LAYER, planes, plane)
    ship_couple(1)
    ship_couple(2)
    gather_cross(2)
    build_gt(0)
    add_cross(1)

    for level in range(3):
        g = size[level]
        gp = size[level + 1]
        nch = gp // g
        child_me = me % gp // g
        need((N_SRC, level + 1))
        name = (N_F1, N_F2, N_F3B)[level]
        buf, step = m[name], g
        if level == 2:
            step = g // plane
        arrive(name, gp if level < 2 else planes)
        ws = [
            jnp.sum(buf[child * step : (child + 1) * step, :count, :], axis=0) * mask(N_KID, level, child, 1)
            for child in range(nch)
        ]
        ws = jnp.concatenate(ws, axis=1)
        bn = src[level + 1][...]
        upd = 0.0
        if level == 0:
            inc = by_halves(ws, (N_GTH, 0), 0)
            bn = bn - inc[:, :LANES]
            upd = -inc[:, LANES:]
        elif level == 1:
            rows = jnp.concatenate([buf[j, count : 2 * count, :] for j in range(gp)], axis=1)
            inc = select(rows, m[N_BOT_MIDDLE][...], 1)
            bn = jnp.concatenate([bn + inc[:, :LANES], ws], axis=1)
            upd = inc[:, LANES:] - by_halves(ws, (N_GTH, 1), 0, slice(LANES, 2 * LANES))
        else:
            bn = jnp.concatenate([bn + jnp.sum(buf[:, count : 2 * count, :], axis=0), ws], axis=1)
        local_n, bq, *sent = local_forward(level + 1, bn)
        if level < 2:
            sent.append(upd)
        else:
            sent = [bq] + sent[:1] + sent[2:] + sent[1:2]
        name = (N_F2, N_F3A, N_F4A)[level]
        group = size[2] if level == 0 else plane
        m[name][me % group] = jnp.concatenate(sent, axis=0)
        send_all(name, group)
        if level < 2:
            m[N_HQ, level + 1][me % gp] = bq
            send_all((N_HQ, level + 1), gp)
        if level > 0:
            arrive((N_HQ, level), g)
            hq = jnp.sum(m[N_HQ, level][...], axis=0) * mask(N_OWN, level, 0)
            z = (local + outer(hq, exp[level][...])) * piv[level][...]
            m[N_Z, level][...] = z
            share(level, mult(z, exp[level][...]))
        local = local_n
        if level == 0:
            build_forward(2)
            fill_masks(2)
            build_forward(3)
            scatter_cross(3)
            build_gt(1)
            build_bot_middle()
            add_cross(2)
            chain_forward(2)
        elif level == 1:
            build_gt(2)
            g_scatter()
            reply_rows()
            build_bot_upper()
            fill_masks(3)
            arrive(N_F3A, plane)
            sums = jnp.sum(m[N_F3A][:, :count, :], axis=0)
            rows = jnp.concatenate([m[N_F3A][j, count:, :] for j in range(plane)], axis=1)
            part = select(rows, m[N_BOT_UPPER][...], 1)
            for q in range(planes):
                m[N_F3S][q] = jnp.concatenate([sums, part[:, q * LANES : (q + 1) * LANES]], axis=0)
            m[N_F3B][layer] = m[N_F3S][layer]
            send_each(lambda q: m[N_F3S].at[q], lambda i: m[N_F3B].at[i], planes, N_F3B, plane)
            pending.append((m[N_F3S].at[pl.ds(0, planes - 1)], sem_of(N_F3B)))
            put_halves((N_FWD, 3), 4 * RANK, outer(m[N_NEAR][...], m[N_GT, 2][...]))
            chain_forward(3)
            share(0, mult(m[N_Z, 0][...], exp[0][...]))
            start_cross(0)
            m[N_LAST, 0][...] = mult(blk[0][...], bas[0][:, RANK:])
            build_ft_upper()
            if not late:
                build_ft_middle()
            cross_planes()
        else:
            g_across()

    gather_cross(3)
    gather_cross(0)
    arrive(N_F4A, plane)
    o = (2 + size[3] // size[2]) * count
    sums = jnp.sum(m[N_F4A][:, :o, :], axis=0)
    rows = jnp.concatenate([m[N_F4A][j, o:, :] for j in range(plane)], axis=1)
    part = select(rows, m[N_FT_UPPER][...], 0)
    for q in range(planes):
        c = 2 + q * plane // size[2]
        m[N_F4S][q] = jnp.concatenate(
            [sums[: 2 * count], sums[c * count : (c + 1) * count], part[:, q * LANES : (q + 1) * LANES]], axis=0
        )
    m[N_F4B][layer] = m[N_F4S][layer]
    send_each(lambda q: m[N_F4S].at[q], lambda i: m[N_F4B].at[i], planes, N_F4B, plane)
    pending.append((m[N_F4S].at[pl.ds(0, planes - 1)], sem_of(N_F4B)))
    g_gather()
    build_named()
    prepare_back(2)
    arrive_cross(3)
    arrive(N_F4B, planes)
    g_arrive()
    both = jnp.sum(m[N_F4B][...], axis=0)
    hq = both[:count] * mask(N_OWN, 3, 0)
    rp = (both[count : 2 * count] + mult(hq, m[N_CROSS, 3][...].reshape(RANK, RANK))) * mask(N_OWN, 3, 0)
    pair = jnp.concatenate([rp, hq], axis=1)
    s = both[2 * count : 3 * count] + by_halves(pair, N_GH, 1)
    xu = both[3 * count :] + by_halves(pair, N_NAMED, 0)

    for level in (2, 1, 0):
        s = s * mask(N_OWN, level, 1)
        xs = m[N_XZ, level][...] - by_halves(s, (N_BACK, level), 1)
        x = xs[:, :LANES]
        if level == 0:
            outs[0][...] = x
            break
        g = size[level - 1]
        gp = size[level]
        nch = gp // g
        place = me % gp
        child_me = place // g
        sp = xs[:, LANES:] + by_halves(xu, (N_GTH, level - 1), 1, slice(LANES, 2 * LANES))
        name = (N_B3, N_B2)[level - 1]
        buf, piece = m[name], m[N_PIECE, level - 1]
        for c in range(nch):
            piece[c] = sp[:, c * RANK : (c + 1) * RANK] if level == 1 else jnp.concatenate(
                [sp[:, c * RANK : (c + 1) * RANK], x, xu], axis=0
            )
        buf[place] = piece[child_me]
        send_each(lambda q: piece.at[lax.div(q, g)], lambda i: buf.at[i], gp, name)
        pending.append((buf.at[pl.ds(0, gp - 1)], sem_of(name)))
        outs[level][...] = x
        if level == 2:
            z = (local + outer(hq, exp[3][...])) * piv[3][...]
            outs[3][...] = outer(z, blk[3][...]) + outer(rp, bas[3][:, :RANK])
        else:
            add_cross(0)
        prepare_back(level - 1)
        arrive(name, gp)
        s = jnp.sum(buf[:, :count, :], axis=0)
        if level == 2:
            blocks = [buf[j, count : 2 * count, :] for j in range(gp)]
            blocks += [buf[j, 2 * count :, :] for j in range(gp)]
            if late:
                build_ft_middle()
            xu = select(jnp.concatenate(blocks, axis=1), m[N_FT_MIDDLE][...], 0)

    if shared_sends:
        assert all(group_of(level) == parts_of[level] for level in range(4))
        wait_rows(sum(sent_rows) + sum(rows_in(part) for part, _ in pending), send_sem.at[0])
    else:
        for part, sem in pending:
            wait_for(part, send_sem.at[sem])
        for level in range(4):
            g = group_of(level)
            p = parts_of[level]
            rp = RANK // p
            gp = spread_of(level)
            n = gp // g * p
            idx = me % g
            rs_sem = send_sem.at[sem_of((N_RS, level))]
            ag_sem = send_sem.at[sem_of((N_CROSS, level))]
            cross_p, buf = m[N_CROSS_P, level], m[N_CROSS, level]

            def ag_done():
                for _ in range((gp - 1) // n):
                    wait_for(buf.at[pl.ds(0, n)], ag_sem)
                if (gp - 1) % n:
                    wait_for(buf.at[pl.ds(0, (gp - 1) % n)], ag_sem)
                if level == 3:
                    wait_for(m[N_GRAM].at[pl.ds(0, planes - 1)], send_sem.at[sem_of(N_GRAM)])

            if g == p:
                wait_for(cross_p.at[pl.ds(0, (p - 1) * rp)], rs_sem)
                ag_done()
            else:
                pl.when(idx < p)(lambda: wait_for(cross_p.at[pl.ds(0, (p - 1) * rp)], rs_sem))
                pl.when(idx >= p)(lambda: wait_for(cross_p, rs_sem))
                pl.when(idx < p)(ag_done)
        g_drain()


def put_out(*refs):
    n = len(refs) // 2
    ins, outs, sem = refs[:n], refs[n : 2 * n], refs[-1]
    copies = [pltpu.make_async_copy(ins[i], outs[i], sem.at[i]) for i in range(n)]
    for c in copies:
        c.start()
    for c in copies:
        c.wait()


def solution(mesh):
    leaves, across = mesh.shape["leaf"], mesh.shape["grid"]

    def shards(*args):
        levels = [args[8 * i : 8 * i + 8] for i in range(3)]
        root = args[24:30]
        (sl, bl, el, qs, pv, cl, rk, tg) = zip(*levels)
        src = list(sl) + [root[0]]
        blk = list(bl) + [root[1]]
        exp = list(el) + [root[2]]
        bas = list(qs) + [root[3]]
        piv = [v.reshape(1, -1) for v in list(pv) + [root[4]]]
        rnk = list(rk) + [root[5]]
        tgt = [t.reshape(1, -1) for t in tg]
        count = src[0].shape[0]
        ups = [t.shape[1] for t in tgt]
        fronts = [r.shape[0] for r in rnk]
        rnk = [r.T if r.shape[0] > 2 else r for r in rnk]
        size = [leaves * across // f for f in fronts]
        for v in src:
            assert v.shape[1] == LANES
        vm = lambda *s: pltpu.VMEM(s, F32)
        bits = lambda *s: pltpu.VMEM(s, BF16)
        total = leaves * across
        plane = size[1]
        planes = total // plane
        nch = [size[i + 1] // size[i] for i in range(3)]
        caps = [max(1, -(-ups[i] // size[i + 1])) for i in range(3)]
        group = size[:3] + [plane]
        spread = group
        parts = [min(g, 16) for g in group]
        ft = (size[2] * 2 * LANES, LANES)
        bufs = {
            N_F0: vm(size[0], count, LANES),
            N_F1: vm(plane, count, LANES),
            N_F2: vm(size[2], 2 * count, LANES),
            N_F3A: vm(plane, 2 * count, LANES),
            N_F3S: vm(planes, 2 * count, LANES),
            N_F3B: vm(planes, 2 * count, LANES),
            (N_HQ, 1): vm(size[1], count, LANES),
            (N_HQ, 2): vm(size[2], count, LANES),
            N_F4A: vm(plane, (nch[2] + 3) * count, LANES),
            N_F4S: vm(planes, 4 * count, LANES),
            N_F4B: vm(planes, 4 * count, LANES),
            N_NEAR: vm(LANES, LANES),
            N_RULER: vm(8192 if total <= 64 else 1024, LANES),
            (N_HIT, 0): bits(total * 8, LANES),
            (N_HIT, 1): bits(total * 8, LANES),
            N_ROWS_S: vm(total, 8, LANES),
            N_ROWS_R: vm(total, 8, LANES),
            (N_NAMED, 0): bits(2 * RANK, LANES),
            (N_NAMED, 1): bits(2 * RANK, LANES),
            (N_GH, 0): bits(RANK, 2 * RANK),
            (N_GH, 1): bits(RANK, 2 * RANK),
            N_G_P: vm(parts[3], nch[2] * RANK // parts[3], 2 * RANK),
            N_G_RS: vm(plane, nch[2] * RANK // parts[3], 2 * RANK),
            N_G_ZS: vm(nch[2], RANK // parts[3], 2 * RANK),
            N_G_Z: vm(planes, RANK // parts[3], 2 * RANK),
            N_G: vm(parts[3], RANK // parts[3], 2 * RANK),
            N_B2: vm(size[2], 3 * count, LANES),
            N_B3: vm(size[1], count, LANES),
            N_TGT_MIDDLE: vm(size[2], 1, LANES),
            N_TGT_UPPER: vm(plane, 1, LANES),
            N_TGT_LAYER: vm(planes, 1, LANES),
            N_BOT_MIDDLE: bits(2 * LANES, size[2] * LANES),
            N_BOT_UPPER: bits(planes * LANES, plane * LANES),
            N_FT_MIDDLE: bits(*ft),
            N_FT_UPPER: bits(plane * LANES, planes * LANES),
            N_MASK: vm(6 + 2 * sum(nch), count, LANES),
            N_GRAM: vm(planes, RANK // parts[3], RANK),
        }
        arrays = {N_SRC: src, N_BLK: blk, N_EXP: exp, N_BAS: bas, N_PIV: piv, N_RNK: rnk, N_CPL: cl, N_TGT: tgt}
        for name, list_of in arrays.items():
            for i, v in enumerate(list_of):
                bufs[name, i] = pltpu.VMEM(v.shape, v.dtype)
        for i in range(4):
            bufs[N_LAST, i] = vm(LANES, RANK)
            for j in range(2):
                if i > 0:
                    bufs[(N_FWD, i), j] = bits(LANES + (nch[i - 1] * RANK if i > 1 else 0), (3 if i < 3 else 4 + nch[2]) * RANK)
                if i < 3:
                    bufs[(N_BACK, i), j] = bits((1 + (nch[i - 1] if i > 0 else 0)) * RANK, RANK)
        for i in range(2):
            for j in range(2):
                bufs[(N_GTH, i), j] = bits(nch[i] * RANK, 2 * LANES)
        for i in range(3):
            bufs[N_Z, i] = vm(count, LANES)
            bufs[N_XZ, i] = vm(count, (1 + (nch[i - 1] if i > 0 else 0)) * LANES)
        for i in range(4):
            bufs[N_CROSS_P, i] = vm(RANK, RANK)
            bufs[N_RS, i] = vm(group[i], RANK // parts[i], RANK)
            bufs[N_CROSS, i] = vm(spread[i] // group[i] * parts[i], RANK // parts[i], RANK)
        for i in range(3):
            wide = max(8, -(-caps[i] // 8) * 8)
            assert caps[i] <= 4 or size[i] * wide <= LANES
            if caps[i] == wide:
                bufs[N_LOW_S, i] = vm(size[i + 1], 1, LANES)
                bufs[N_LOW, i] = vm(size[i + 1], 1, LANES)
            bufs[N_PERM, i] = vm(size[i + 1], wide, LANES)
            bufs[N_COUPLE, i] = vm(size[i + 1], wide, LANES)
            bufs[N_GT, i] = vm(nch[i] * RANK, LANES * (1 if i == 2 else 2))
            bufs[N_ZP, i] = vm(size[i], count, LANES)
            bufs[N_PIECE, i] = vm(nch[i], (1 if i == 0 else 3) * count, LANES)
        scratch = list(bufs.values())
        scratch += [pltpu.SemaphoreType.DMA((n,)) for n in (1 if total <= 64 else 37, 37, 11)]
        scratch += [pltpu.SemaphoreType.REGULAR]
        vspec = pl.BlockSpec(memory_space=pltpu.VMEM)
        aspec = pl.BlockSpec(memory_space=pl.ANY)
        answers = pl.pallas_call(
            functools.partial(kernel, (leaves, across, size, ups, count, caps, fronts), list(bufs)),
            out_shape=[pltpu.VMEM(v.shape, F32) for v in src],
            in_specs=[aspec] * 30,
            out_specs=[vspec] * 4,
            scratch_shapes=scratch,
            compiler_params=pltpu.CompilerParams(
                collective_id=0, has_side_effects=True, vmem_limit_bytes=63 * 1024 * 1024
            ),
        )(*src, *blk, *exp, *bas, *piv, *rnk, *cl, *tgt)
        return pl.pallas_call(
            put_out,
            out_shape=[jax.ShapeDtypeStruct(v.shape, F32) for v in src],
            in_specs=[vspec] * 4,
            out_specs=[aspec] * 4,
            scratch_shapes=[pltpu.SemaphoreType.DMA((4,))],
        )(*[pltpu.with_memory_space_constraint(v, pltpu.VMEM) for v in answers])

    spread_axes = ("leaf", "grid")
    level = (P(None, spread_axes), P(spread_axes, None), P(spread_axes, None), P(spread_axes, None), P(spread_axes))
    mid = level + (P(spread_axes, None), P(), P(spread_axes))
    return jax.shard_map(
        shards,
        mesh=mesh,
        in_specs=mid * 3 + level + (P(),),
        out_specs=(P(None, spread_axes),) * 4,
        check_vma=False,
    )
```

time: 56.6 us -> 45 us (0.80)
  Pallas kernels: 55.7 us -> 44.2 us
    pallas_call x1, Pallas kernels: 55.1 us -> 43.5 us  [shards(): pl.pallas_call(functools.partial(kernel, (leaves, across, size, ups, coun...]
where the time goes in v2:
time: 45 us; the launch traced here: 44.8 us
  Pallas kernels  44.2 us (98%)
  between operations  0.65 us (1%)
    pallas_call x1, Pallas kernels, shards(): pl.pallas_call(functools.partial(kernel, (leaves, across, size, ups, coun...  43.5 us

profile of v2, /device:TPU:0, one launch (start us, length us, event | category | flops | bytes accessed | tf_op | source)
XLA Modules:
  0.0 44.8 jit_solution(7939843769537560400)
XLA Ops:
  0.6 43.5 %shard_map.309 = (f32[8,128]{1,0:T(8,128)S(1)}, f32[8,128]{1,0:T(8,128)S(1)}, f32[8,128]{1,0:T(8,128)S(1)}, f32[8,128]{1,0:T(8,128)S(1)}) custom-call(f32[8,128]{1,0:T(8,128)} %refs_0_.1, f32[8,128]{1,0:T(8,128)} %refs_1_.1, f32[8,128]{1,0:T(8,128)} %refs_2_.1, f32[8,128]{1,0:T(8,128)} %refs_3_.1, f32[128,128]{1,0:T(8,128)} %refs_4_.1, f32[128,128]{1,0:T(8,128)} %refs_5_.1, ...), custom_call_target="tpu_custom_call" | custom-call | tf_op jit(solution)/shard_map/pallas_call | solution.py:1034
  44.2 0.6 %shard_map.310 = (f32[8,128]{1,0:T(8,128)}, f32[8,128]{1,0:T(8,128)}, f32[8,128]{1,0:T(8,128)}, f32[8,128]{1,0:T(8,128)}) custom-call(f32[8,128]{1,0:T(8,128)S(1)} %get-tuple-element.8.refs_0_, f32[8,128]{1,0:T(8,128)S(1)} %get-tuple-element.9.refs_1_, f32[8,128]{1,0:T(8,128)S(1)} %get-tuple-element.10.refs_2_, f32[8,128]{1,0:T(8,128)S(1)} %get-tuple-element.11.refs_3_), custom_call_target="tpu_custom_call" | custom-call | tf_op jit(solution)/shard_map/pallas_call | solution.py:1044

commit v3 on v2

--- a/solution.py
+++ b/solution.py
@@ -13,14 +13,15 @@
 MESH = pl.DeviceIdType.MESH
 F32 = jnp.float32
 BF16 = jnp.bfloat16
+F8 = jnp.float8_e4m3fn
 
 (
     N_SRC, N_BLK, N_EXP, N_BAS, N_PIV, N_RNK, N_CPL, N_TGT, N_RULER, N_COUPLE, N_MASK, N_OWN, N_KID,
-    N_CROSS_P, N_LAST, N_NEAR, N_FWD, N_GT, N_CROSS, N_RS, N_GRAM, N_PERM, N_HIT, N_LOW_S, N_LOW, N_GTH,
-    N_ROWS_S, N_ROWS_R, N_NAMED, N_G_P, N_G_RS, N_G_ZS, N_G_Z, N_G, N_GH, N_Z, N_XZ, N_BACK, N_TGT_MIDDLE,
-    N_BOT_MIDDLE, N_TGT_UPPER, N_BOT_UPPER, N_FT_MIDDLE, N_TGT_LAYER, N_FT_UPPER, N_ZP, N_F0, N_F1, N_F2,
-    N_F3B, N_F3A, N_F4A, N_HQ, N_F3S, N_F4S, N_F4B, N_B3, N_B2, N_PIECE,
-) = range(59)
+    N_CROSS_P, N_LAST, N_NEAR, N_FWD, N_GT, N_CROSS, N_RS, N_GRAM, N_PERM, N_TAKE_KEY, N_HIT, N_LOW_S, N_LOW,
+    N_OT, N_GTH, N_ROWS_S, N_ROWS_R, N_NAMED, N_G_P, N_G_RS, N_G_ZS, N_G_Z, N_G, N_GH, N_Z, N_XZ, N_BACK,
+    N_TGT_MIDDLE, N_BOT_MIDDLE, N_TGT_UPPER, N_BOT_UPPER, N_TAKE, N_FT_MIDDLE, N_TGT_LAYER, N_FT_UPPER, N_ZP,
+    N_F0, N_F1, N_F2, N_F3B, N_F3A, N_F4A, N_HQ, N_F3S, N_F4S, N_F4B, N_B3, N_B2, N_PIECE,
+) = range(62)
 
 
 def once(a, b, ca, cb):
@@ -83,7 +84,6 @@
     planes = total_devices // plane
     spot = me % plane
     layer = me // plane
-    late = total_devices > 64
     pending = []
 
     shared_sends = total_devices <= 64
@@ -345,17 +345,19 @@
 
         holds_part(level, go)
 
+    def wide_of(level):
+        return max(8, -(-caps[level] // 8) * 8)
+
     def rows_path(level):
         return size[level] * wide_of(level) <= LANES
 
+    by_slots = size[2] * wide_of(1) <= LANES
+
     def tucked(level):
         return caps[level] < wide_of(level)
 
     def couple_rows(level):
         return caps[level] + 1 if rows_path(level) and tucked(level) else wide_of(level)
-
-    def wide_of(level):
-        return max(8, -(-caps[level] // 8) * 8)
 
     def make_couple(level):
         need((N_TGT, level), (N_CPL, level))
@@ -383,6 +385,8 @@
         moved = sum(once(hit16, piece, 1, 0) for piece in halves(cpl[level][...]))
         perm_buf, recv_c = m[N_PERM, level], m[N_COUPLE, level]
         idx = me % gp
+        if level == 1 and by_slots:
+            m[N_TAKE_KEY][...] = (dst * LANES + me % gp * wide + rank).astype(F32)
         if level == 2:
             m[N_HIT, 0][...] = hit16
             m[N_HIT, 1][...] = (si == pos + 4).astype(F32).astype(BF16)
@@ -461,6 +465,8 @@
                 ri = lax.broadcasted_iota(jnp.int32, (rows, slots), 0).astype(F32)
                 ot = (ri == low_row(level, child)).astype(F32).astype(BF16)
                 full = sum(once(piece, ot, 0, 1) for piece in halves(got))
+                if level == 1 and by_slots:
+                    m[N_OT][:, child * slots : (child + 1) * slots] = ot.astype(F8)
             else:
                 lane = lax.broadcasted_iota(jnp.int32, (slots, rows), 1).astype(F32)
                 ot = (lane == low_column(level, child)[0]).astype(F32).astype(BF16)
@@ -514,7 +520,7 @@
         else:
             pl.when(spot < g_p)(go)
 
-    def g_scatter():
+    def g_make():
         both = jnp.concatenate([bas[3][:, :RANK], m[N_LAST, 3][...]], axis=1)
         full = mult(m[N_GT, 2][...], both)
         n = full.shape[0] // RANK
@@ -522,6 +528,8 @@
             m[N_G_P][j] = jnp.concatenate(
                 [full[c * RANK + j * g_rp : c * RANK + (j + 1) * g_rp] for c in range(n)], axis=0
             )
+
+    def g_scatter():
         sem = sem_of(N_G_RS)
 
         def body(k, carry):
@@ -632,7 +640,7 @@
         def fill(j, carry):
             t = m[N_TGT_MIDDLE][j]
             lanes = pl.ds(pl.multiple_of(j * LANES, LANES), LANES)
-            m[N_BOT_MIDDLE][:, lanes] = (mine == t).astype(F32).astype(BF16)
+            m[N_BOT_MIDDLE][:, lanes] = (mine == t).astype(F32).astype(F8)
             return carry
 
         lax.fori_loop(0, gp, fill, 0)
@@ -646,10 +654,21 @@
         def fill(j, carry):
             t = m[N_TGT_UPPER][j]
             lanes = pl.ds(pl.multiple_of(j * LANES, LANES), LANES)
-            m[N_BOT_UPPER][:, lanes] = (mine == t).astype(F32).astype(BF16)
+            m[N_BOT_UPPER][:, lanes] = (mine == t).astype(F32).astype(F8)
             return carry
 
         lax.fori_loop(0, plane, fill, 0)
+
+    def build_take():
+        key = m[N_TAKE_KEY][...]
+        ri = lax.broadcasted_iota(jnp.int32, (LANES, LANES), 0)
+
+        def fill(j, carry):
+            rows = pl.ds(pl.multiple_of(j * LANES, LANES), LANES)
+            m[N_TAKE][rows, :] = ((ri + j * LANES).astype(F32) == key).astype(F32).astype(F8)
+            return carry
+
+        lax.fori_loop(0, size[2], fill, 0)
 
     def build_ft_middle():
         t = tgt[1][...]
@@ -657,7 +676,7 @@
 
         def fill(j, carry):
             rows = pl.ds(pl.multiple_of(j * LANES, LANES), LANES)
-            m[N_FT_MIDDLE][rows, :] = (ri + j * LANES == t).astype(F32).astype(BF16)
+            m[N_FT_MIDDLE][rows, :] = (ri + j * LANES == t).astype(F32).astype(F8)
             return carry
 
         lax.fori_loop(0, m[N_FT_MIDDLE].shape[0] // LANES, fill, 0)
@@ -670,7 +689,7 @@
         def fill(j, carry):
             rows = pl.ds(pl.multiple_of(j * LANES, LANES), LANES)
             here = ((ri + (layer * plane + j) * LANES).astype(F32) == t).astype(F32)
-            m[N_FT_UPPER][rows, :] = here.astype(BF16)
+            m[N_FT_UPPER][rows, :] = here.astype(F8)
             return carry
 
         lax.fori_loop(0, plane, fill, 0)
@@ -769,6 +788,10 @@
         if level < 2:
             m[N_HQ, level + 1][me % gp] = bq
             send_all((N_HQ, level + 1), gp)
+        if level == 1:
+            g_scatter()
+        if level == 2:
+            g_across()
         if level > 0:
             arrive((N_HQ, level), g)
             hq = jnp.sum(m[N_HQ, level][...], axis=0) * mask(N_OWN, level, 0)
@@ -785,9 +808,9 @@
             build_bot_middle()
             add_cross(2)
             chain_forward(2)
+            build_gt(2)
+            g_make()
         elif level == 1:
-            build_gt(2)
-            g_scatter()
             reply_rows()
             build_bot_upper()
             fill_masks(3)
@@ -806,14 +829,12 @@
             start_cross(0)
             m[N_LAST, 0][...] = mult(blk[0][...], bas[0][:, RANK:])
             build_ft_upper()
-            if not late:
-                build_ft_middle()
+            if by_slots:
+                build_take()
             cross_planes()
-        else:
-            g_across()
-
     gather_cross(3)
     gather_cross(0)
+    g_gather()
     arrive(N_F4A, plane)
     o = (2 + size[3] // size[2]) * count
     sums = jnp.sum(m[N_F4A][:, :o, :], axis=0)
@@ -827,7 +848,6 @@
     m[N_F4B][layer] = m[N_F4S][layer]
     send_each(lambda q: m[N_F4S].at[q], lambda i: m[N_F4B].at[i], planes, N_F4B, plane)
     pending.append((m[N_F4S].at[pl.ds(0, planes - 1)], sem_of(N_F4B)))
-    g_gather()
     build_named()
     prepare_back(2)
     arrive_cross(3)
@@ -856,9 +876,12 @@
         name = (N_B3, N_B2)[level - 1]
         buf, piece = m[name], m[N_PIECE, level - 1]
         for c in range(nch):
-            piece[c] = sp[:, c * RANK : (c + 1) * RANK] if level == 1 else jnp.concatenate(
-                [sp[:, c * RANK : (c + 1) * RANK], x, xu], axis=0
-            )
+            rest = []
+            if level == 2 and by_slots:
+                rest = [select(jnp.concatenate([x, xu], axis=1), m[N_OT][...], 0)]
+            elif level == 2:
+                rest = [x, xu]
+            piece[c] = jnp.concatenate([sp[:, c * RANK : (c + 1) * RANK]] + rest, axis=0)
         buf[place] = piece[child_me]
         send_each(lambda q: piece.at[lax.div(q, g)], lambda i: buf.at[i], gp, name)
         pending.append((buf.at[pl.ds(0, gp - 1)], sem_of(name)))
@@ -873,10 +896,10 @@
         s = jnp.sum(buf[:, :count, :], axis=0)
         if level == 2:
             blocks = [buf[j, count : 2 * count, :] for j in range(gp)]
-            blocks += [buf[j, 2 * count :, :] for j in range(gp)]
-            if late:
+            if not by_slots:
+                blocks += [buf[j, 2 * count :, :] for j in range(gp)]
                 build_ft_middle()
-            xu = select(jnp.concatenate(blocks, axis=1), m[N_FT_MIDDLE][...], 0)
+            xu = select(jnp.concatenate(blocks, axis=1), m[N_TAKE if by_slots else N_FT_MIDDLE][...], 0)
 
     if shared_sends:
         assert all(group_of(level) == parts_of[level] for level in range(4))
@@ -946,6 +969,7 @@
             assert v.shape[1] == LANES
         vm = lambda *s: pltpu.VMEM(s, F32)
         bits = lambda *s: pltpu.VMEM(s, BF16)
+        ones = lambda *s: pltpu.VMEM(s, F8)
         total = leaves * across
         plane = size[1]
         planes = total // plane
@@ -954,7 +978,7 @@
         group = size[:3] + [plane]
         spread = group
         parts = [min(g, 16) for g in group]
-        ft = (size[2] * 2 * LANES, LANES)
+        by_slots = size[2] * max(8, -(-caps[1] // 8) * 8) <= LANES
         bufs = {
             N_F0: vm(size[0], count, LANES),
             N_F1: vm(plane, count, LANES),
@@ -982,15 +1006,14 @@
             N_G_ZS: vm(nch[2], RANK // parts[3], 2 * RANK),
             N_G_Z: vm(planes, RANK // parts[3], 2 * RANK),
             N_G: vm(parts[3], RANK // parts[3], 2 * RANK),
-            N_B2: vm(size[2], 3 * count, LANES),
+            N_B2: vm(size[2], (2 if by_slots else 3) * count, LANES),
             N_B3: vm(size[1], count, LANES),
             N_TGT_MIDDLE: vm(size[2], 1, LANES),
             N_TGT_UPPER: vm(plane, 1, LANES),
             N_TGT_LAYER: vm(planes, 1, LANES),
-            N_BOT_MIDDLE: bits(2 * LANES, size[2] * LANES),
-            N_BOT_UPPER: bits(planes * LANES, plane * LANES),
-            N_FT_MIDDLE: bits(*ft),
-            N_FT_UPPER: bits(plane * LANES, planes * LANES),
+            N_BOT_MIDDLE: ones(2 * LANES, size[2] * LANES),
+            N_BOT_UPPER: ones(planes * LANES, plane * LANES),
+            N_FT_UPPER: ones(plane * LANES, planes * LANES),
             N_MASK: vm(6 + 2 * sum(nch), count, LANES),
             N_GRAM: vm(planes, RANK // parts[3], RANK),
         }
@@ -1005,6 +1028,12 @@
                     bufs[(N_FWD, i), j] = bits(LANES + (nch[i - 1] * RANK if i > 1 else 0), (3 if i < 3 else 4 + nch[2]) * RANK)
                 if i < 3:
                     bufs[(N_BACK, i), j] = bits((1 + (nch[i - 1] if i > 0 else 0)) * RANK, RANK)
+        if by_slots:
+            bufs[N_TAKE_KEY] = vm(1, LANES)
+            bufs[N_TAKE] = ones(size[2] * LANES, LANES)
+            bufs[N_OT] = ones(2 * LANES, LANES)
+        else:
+            bufs[N_FT_MIDDLE] = ones(size[2] * 2 * LANES, LANES)
         for i in range(2):
             for j in range(2):
                 bufs[(N_GTH, i), j] = bits(nch[i] * RANK, 2 * LANES)
@@ -1025,7 +1054,7 @@
             bufs[N_COUPLE, i] = vm(size[i + 1], wide, LANES)
             bufs[N_GT, i] = vm(nch[i] * RANK, LANES * (1 if i == 2 else 2))
             bufs[N_ZP, i] = vm(size[i], count, LANES)
-            bufs[N_PIECE, i] = vm(nch[i], (1 if i == 0 else 3) * count, LANES)
+            bufs[N_PIECE, i] = vm(nch[i], (1 if i == 0 else 2 if by_slots else 3) * count, LANES)
         scratch = list(bufs.values())
         scratch += [pltpu.SemaphoreType.DMA((n,)) for n in (1 if total <= 64 else 37, 37, 11)]
         scratch += [pltpu.SemaphoreType.REGULAR]

time: 45 us -> 43.5 us (0.967)
  Pallas kernels: 44.2 us -> 42.7 us
    pallas_call x1, Pallas kernels: 43.5 us -> 42.1 us  [shards(): pl.pallas_call(functools.partial(kernel, (leaves, across, size, ups, coun...]
where the time goes in v3:
time: 43.5 us; the launch traced here: 43.4 us
  Pallas kernels  42.7 us (98%)
  between operations  0.65 us (1%)
    pallas_call x1, Pallas kernels, shards(): pl.pallas_call(functools.partial(kernel, (leaves, across, size, ups, coun...  42.1 us

profile of v3, /device:TPU:0, one launch (start us, length us, event | category | flops | bytes accessed | tf_op | source)
XLA Modules:
  0.0 43.4 jit_solution(3743642205867872798)
XLA Ops:
  0.6 42.1 %shard_map.309 = (f32[8,128]{1,0:T(8,128)S(1)}, f32[8,128]{1,0:T(8,128)S(1)}, f32[8,128]{1,0:T(8,128)S(1)}, f32[8,128]{1,0:T(8,128)S(1)}) custom-call(f32[8,128]{1,0:T(8,128)} %refs_0_.1, f32[8,128]{1,0:T(8,128)} %refs_1_.1, f32[8,128]{1,0:T(8,128)} %refs_2_.1, f32[8,128]{1,0:T(8,128)} %refs_3_.1, f32[128,128]{1,0:T(8,128)} %refs_4_.1, f32[128,128]{1,0:T(8,128)} %refs_5_.1, ...), custom_call_target="tpu_custom_call" | custom-call | tf_op jit(solution)/shard_map/pallas_call | solution.py:1063
  42.7 0.6 %shard_map.310 = (f32[8,128]{1,0:T(8,128)}, f32[8,128]{1,0:T(8,128)}, f32[8,128]{1,0:T(8,128)}, f32[8,128]{1,0:T(8,128)}) custom-call(f32[8,128]{1,0:T(8,128)S(1)} %get-tuple-element.8.refs_0_, f32[8,128]{1,0:T(8,128)S(1)} %get-tuple-element.9.refs_1_, f32[8,128]{1,0:T(8,128)S(1)} %get-tuple-element.10.refs_2_, f32[8,128]{1,0:T(8,128)S(1)} %get-tuple-element.11.refs_3_), custom_call_target="tpu_custom_call" | custom-call | tf_op jit(solution)/shard_map/pallas_call | solution.py:1073

commit v4 on v3

--- a/solution.py
+++ b/solution.py
@@ -11,6 +11,7 @@
 RANK = 128
 LANES = 128
 MESH = pl.DeviceIdType.MESH
+NSEM = 36
 F32 = jnp.float32
 BF16 = jnp.bfloat16
 F8 = jnp.float8_e4m3fn
@@ -20,8 +21,8 @@
     N_CROSS_P, N_LAST, N_NEAR, N_FWD, N_GT, N_CROSS, N_RS, N_GRAM, N_PERM, N_TAKE_KEY, N_HIT, N_LOW_S, N_LOW,
     N_OT, N_GTH, N_ROWS_S, N_ROWS_R, N_NAMED, N_G_P, N_G_RS, N_G_ZS, N_G_Z, N_G, N_GH, N_Z, N_XZ, N_BACK,
     N_TGT_MIDDLE, N_BOT_MIDDLE, N_TGT_UPPER, N_BOT_UPPER, N_TAKE, N_FT_MIDDLE, N_TGT_LAYER, N_FT_UPPER, N_ZP,
-    N_F0, N_F1, N_F2, N_F3B, N_F3A, N_F4A, N_HQ, N_F3S, N_F4S, N_F4B, N_B3, N_B2, N_PIECE,
-) = range(62)
+    N_F0, N_F1, N_F2, N_F3B, N_F2U, N_F3A, N_F4A, N_HQ, N_F3S, N_F4S, N_F4B, N_B3, N_B2, N_PIECE,
+) = range(63)
 
 
 def once(a, b, ca, cb):
@@ -223,6 +224,7 @@
             parts += [m[N_LAST, 3][...], m[N_NEAR][...]]
         else:
             m[N_LAST, level][...] = mult(blk[level][...], bas[level][:, RANK:])
+            parts += [m[N_LAST, level][...]]
         put_halves((N_FWD, level), 0, jnp.concatenate(parts, axis=1))
 
     def put_halves(name, start, value, first=0):
@@ -237,12 +239,11 @@
         put_halves((N_FWD, level), 0, -mult(m[N_GT, level - 1][:, :LANES], top), LANES)
 
     def add_cross(level):
-        arrive_cross(level)
+        if level == 0:
+            arrive_cross(0)
         heads = bas[level][:, :RANK] * mask(N_OWN, level, 0)[:1]
         yt = m[N_LAST, level][...] + mult(heads, m[N_CROSS, level][...].reshape(RANK, RANK))
         m[N_LAST, level][...] = yt
-        if level > 0:
-            put_halves((N_FWD, level), 2 * RANK, yt)
 
     def by_halves(a, name, cb, lanes=slice(None)):
         ah, al = halves(a)
@@ -745,7 +746,6 @@
     ship_couple(2)
     gather_cross(2)
     build_gt(0)
-    add_cross(1)
 
     for level in range(3):
         g = size[level]
@@ -757,6 +757,10 @@
         buf, step = m[name], g
         if level == 2:
             step = g // plane
+        if level == 1:
+            arrive(N_F2U, gp)
+            rows = jnp.concatenate([m[N_F2U][j] for j in range(gp)], axis=1)
+            inc = select(rows, m[N_BOT_MIDDLE][...], 1)
         arrive(name, gp if level < 2 else planes)
         ws = [
             jnp.sum(buf[child * step : (child + 1) * step, :count, :], axis=0) * mask(N_KID, level, child, 1)
@@ -764,22 +768,22 @@
         ]
         ws = jnp.concatenate(ws, axis=1)
         bn = src[level + 1][...]
-        upd = 0.0
         if level == 0:
             inc = by_halves(ws, (N_GTH, 0), 0)
-            bn = bn - inc[:, :LANES]
-            upd = -inc[:, LANES:]
+            m[N_F2U][me % size[2]] = -inc[:, LANES:]
+            send_all(N_F2U, size[2])
+            local_n, bq, w = local_forward(1, bn - inc[:, :LANES])
+            arrive_cross(1)
+            sent = [w + mult(bq * mask(N_OWN, 1, 0), m[N_CROSS, 1][...].reshape(RANK, RANK))]
         elif level == 1:
-            rows = jnp.concatenate([buf[j, count : 2 * count, :] for j in range(gp)], axis=1)
-            inc = select(rows, m[N_BOT_MIDDLE][...], 1)
             bn = jnp.concatenate([bn + inc[:, :LANES], ws], axis=1)
             upd = inc[:, LANES:] - by_halves(ws, (N_GTH, 1), 0, slice(LANES, 2 * LANES))
+            local_n, bq, w = local_forward(2, bn)
+            arrive_cross(2)
+            sent = [w + mult(bq * mask(N_OWN, 2, 0), m[N_CROSS, 2][...].reshape(RANK, RANK)), upd]
         else:
             bn = jnp.concatenate([bn + jnp.sum(buf[:, count : 2 * count, :], axis=0), ws], axis=1)
-        local_n, bq, *sent = local_forward(level + 1, bn)
-        if level < 2:
-            sent.append(upd)
-        else:
+            local_n, bq, *sent = local_forward(3, bn)
             sent = [bq] + sent[:1] + sent[2:] + sent[1:2]
         name = (N_F2, N_F3A, N_F4A)[level]
         group = size[2] if level == 0 else plane
@@ -800,18 +804,19 @@
             share(level, mult(z, exp[level][...]))
         local = local_n
         if level == 0:
+            add_cross(1)
             build_forward(2)
             fill_masks(2)
             build_forward(3)
             scatter_cross(3)
             build_gt(1)
             build_bot_middle()
-            add_cross(2)
             chain_forward(2)
             build_gt(2)
             g_make()
         elif level == 1:
             reply_rows()
+            add_cross(2)
             build_bot_upper()
             fill_masks(3)
             arrive(N_F3A, plane)
@@ -934,6 +939,7 @@
                 pl.when(idx >= p)(lambda: wait_for(cross_p, rs_sem))
                 pl.when(idx < p)(ag_done)
         g_drain()
+    assert len(sems) <= NSEM
 
 
 def put_out(*refs):
@@ -982,7 +988,8 @@
         bufs = {
             N_F0: vm(size[0], count, LANES),
             N_F1: vm(plane, count, LANES),
-            N_F2: vm(size[2], 2 * count, LANES),
+            N_F2: vm(size[2], count, LANES),
+            N_F2U: vm(size[2], count, LANES),
             N_F3A: vm(plane, 2 * count, LANES),
             N_F3S: vm(planes, 2 * count, LANES),
             N_F3B: vm(planes, 2 * count, LANES),
@@ -1056,7 +1063,7 @@
             bufs[N_ZP, i] = vm(size[i], count, LANES)
             bufs[N_PIECE, i] = vm(nch[i], (1 if i == 0 else 2 if by_slots else 3) * count, LANES)
         scratch = list(bufs.values())
-        scratch += [pltpu.SemaphoreType.DMA((n,)) for n in (1 if total <= 64 else 37, 37, 11)]
+        scratch += [pltpu.SemaphoreType.DMA((n,)) for n in (1 if total <= 64 else NSEM, NSEM, 11)]
         scratch += [pltpu.SemaphoreType.REGULAR]
         vspec = pl.BlockSpec(memory_space=pltpu.VMEM)
         aspec = pl.BlockSpec(memory_space=pl.ANY)

time: 43.5 us -> 42.9 us (0.986)
  Pallas kernels: 42.7 us -> 42.1 us
    pallas_call x1, Pallas kernels: 42.1 us -> 41.4 us  [shards(): pl.pallas_call(functools.partial(kernel, (leaves, across, size, ups, coun...]
where the time goes in v4:
time: 42.9 us; the launch traced here: 42.7 us
  Pallas kernels  42.1 us (98%)
  between operations  0.65 us (2%)
    pallas_call x1, Pallas kernels, shards(): pl.pallas_call(functools.partial(kernel, (leaves, across, size, ups, coun...  41.4 us

profile of v4, /device:TPU:0, one launch (start us, length us, event | category | flops | bytes accessed | tf_op | source)
XLA Modules:
  0.0 42.7 jit_solution(2331489105558773063)
XLA Ops:
  0.6 41.4 %shard_map.309 = (f32[8,128]{1,0:T(8,128)S(1)}, f32[8,128]{1,0:T(8,128)S(1)}, f32[8,128]{1,0:T(8,128)S(1)}, f32[8,128]{1,0:T(8,128)S(1)}) custom-call(f32[8,128]{1,0:T(8,128)} %refs_0_.1, f32[8,128]{1,0:T(8,128)} %refs_1_.1, f32[8,128]{1,0:T(8,128)} %refs_2_.1, f32[8,128]{1,0:T(8,128)} %refs_3_.1, f32[128,128]{1,0:T(8,128)} %refs_4_.1, f32[128,128]{1,0:T(8,128)} %refs_5_.1, ...), custom_call_target="tpu_custom_call" | custom-call | tf_op jit(solution)/shard_map/pallas_call | solution.py:1070
  42.1 0.6 %shard_map.310 = (f32[8,128]{1,0:T(8,128)}, f32[8,128]{1,0:T(8,128)}, f32[8,128]{1,0:T(8,128)}, f32[8,128]{1,0:T(8,128)}) custom-call(f32[8,128]{1,0:T(8,128)S(1)} %get-tuple-element.8.refs_0_, f32[8,128]{1,0:T(8,128)S(1)} %get-tuple-element.9.refs_1_, f32[8,128]{1,0:T(8,128)S(1)} %get-tuple-element.10.refs_2_, f32[8,128]{1,0:T(8,128)S(1)} %get-tuple-element.11.refs_3_), custom_call_target="tpu_custom_call" | custom-call | tf_op jit(solution)/shard_map/pallas_call | solution.py:1080

commit v5 on v4

--- a/solution.py
+++ b/solution.py
@@ -11,16 +11,16 @@
 RANK = 128
 LANES = 128
 MESH = pl.DeviceIdType.MESH
-NSEM = 36
+NSEM = 34
 F32 = jnp.float32
 BF16 = jnp.bfloat16
 F8 = jnp.float8_e4m3fn
 
 (
-    N_SRC, N_BLK, N_EXP, N_BAS, N_PIV, N_RNK, N_CPL, N_TGT, N_RULER, N_COUPLE, N_MASK, N_OWN, N_KID,
-    N_CROSS_P, N_LAST, N_NEAR, N_FWD, N_GT, N_CROSS, N_RS, N_GRAM, N_PERM, N_TAKE_KEY, N_HIT, N_LOW_S, N_LOW,
-    N_OT, N_GTH, N_ROWS_S, N_ROWS_R, N_NAMED, N_G_P, N_G_RS, N_G_ZS, N_G_Z, N_G, N_GH, N_Z, N_XZ, N_BACK,
-    N_TGT_MIDDLE, N_BOT_MIDDLE, N_TGT_UPPER, N_BOT_UPPER, N_TAKE, N_FT_MIDDLE, N_TGT_LAYER, N_FT_UPPER, N_ZP,
+    N_SRC, N_BLK, N_EXP, N_BAS, N_PIV, N_RNK, N_CPL, N_TGT, N_RULER, N_TGT_MIDDLE, N_TGT_UPPER, N_TGT_LAYER,
+    N_COUPLE, N_MASK, N_OWN, N_KID, N_CROSS_P, N_LAST, N_NEAR, N_FWD, N_GT, N_CROSS, N_RS, N_GRAM, N_PERM,
+    N_TAKE_KEY, N_HIT, N_LOW_S, N_LOW, N_OT, N_GTH, N_ROWS_S, N_ROWS_R, N_NAMED, N_G_P, N_G_RS, N_G_ZS,
+    N_G_Z, N_G, N_GH, N_Z, N_XZ, N_BACK, N_BOT_MIDDLE, N_BOT_UPPER, N_TAKE, N_FT_MIDDLE, N_FT_UPPER, N_ZP,
     N_F0, N_F1, N_F2, N_F3B, N_F2U, N_F3A, N_F4A, N_HQ, N_F3S, N_F4S, N_F4B, N_B3, N_B2, N_PIECE,
 ) = range(63)
 
@@ -91,10 +91,10 @@
     sent_rows = []
     loaded = set()
     order = [[(N_SRC, 0), (N_BAS, 0)], [(N_EXP, 1), (N_BAS, 1)]]
-    order += [[(N_CPL, 0), (N_TGT, 0)], [(N_BLK, 0), (N_EXP, 0), (N_PIV, 0)]]
+    order += [[(N_CPL, 0), (N_TGT, 0), (N_BLK, 0), (N_EXP, 0), (N_PIV, 0)]]
     order += [[(N_RNK, i)] for i in range(4)]
     order += [[(N_BLK, 1), (N_SRC, 1), (N_PIV, 1), (N_CPL, 1), (N_TGT, 1), (N_TGT, 2), (N_CPL, 2)]]
-    order += [[(k, i) for k in (N_EXP, N_BAS, N_BLK, N_SRC, N_PIV)] for i in (2, 3)]
+    order += [[(k, i) for i in (2, 3) for k in (N_EXP, N_BAS, N_BLK, N_SRC, N_PIV)]]
     where_from = {(k, i): hbm[j][i] for j, k in enumerate(KINDS) for i in range(4)}
     for i in range(3):
         where_from[N_CPL, i] = cpl_in[i]
@@ -124,6 +124,7 @@
         return (lax.div(peer, across), lax.rem(peer, across))
 
     def sem_of(name):
+        name = N_TGT_MIDDLE if name in (N_TGT_UPPER, N_TGT_LAYER) else name
         return sems.setdefault(name, len(sems))
 
     def remote(a, b, sem, peer):
@@ -635,7 +636,7 @@
         place = me % gp
         rows = 2 * LANES
         ri = lax.broadcasted_iota(jnp.int32, (rows, LANES), 0)
-        arrive(N_TGT_MIDDLE, gp)
+        wait_rows(gp + plane + planes - 3, recv_sem.at[sem_of(N_TGT_MIDDLE)])
         mine = jnp.where(ri < LANES, place * LANES + ri, (gp + place - 1) * LANES + ri).astype(F32)
 
         def fill(j, carry):
@@ -649,7 +650,6 @@
     def build_bot_upper():
         rows = planes * LANES
         ri = lax.broadcasted_iota(jnp.int32, (rows, LANES), 0)
-        arrive(N_TGT_UPPER, plane)
         mine = ((ri // LANES * plane + spot) * LANES + ri % LANES).astype(F32)
 
         def fill(j, carry):
@@ -683,7 +683,6 @@
         lax.fori_loop(0, m[N_FT_MIDDLE].shape[0] // LANES, fill, 0)
 
     def build_ft_upper():
-        arrive(N_TGT_LAYER, planes)
         t = jnp.concatenate([m[N_TGT_LAYER][j] for j in range(planes)], axis=1)
         ri = lax.broadcasted_iota(jnp.int32, (LANES, planes * LANES), 0)
 
@@ -999,7 +998,7 @@
             N_F4S: vm(planes, 4 * count, LANES),
             N_F4B: vm(planes, 4 * count, LANES),
             N_NEAR: vm(LANES, LANES),
-            N_RULER: vm(8192 if total <= 64 else 1024, LANES),
+            N_RULER: vm(8192 if total <= 64 else 1280, LANES),
             (N_HIT, 0): bits(total * 8, LANES),
             (N_HIT, 1): bits(total * 8, LANES),
             N_ROWS_S: vm(total, 8, LANES),
@@ -1063,7 +1062,7 @@
             bufs[N_ZP, i] = vm(size[i], count, LANES)
             bufs[N_PIECE, i] = vm(nch[i], (1 if i == 0 else 2 if by_slots else 3) * count, LANES)
         scratch = list(bufs.values())
-        scratch += [pltpu.SemaphoreType.DMA((n,)) for n in (1 if total <= 64 else NSEM, NSEM, 11)]
+        scratch += [pltpu.SemaphoreType.DMA((n,)) for n in (1 if total <= 64 else NSEM, NSEM, 9)]
         scratch += [pltpu.SemaphoreType.REGULAR]
         vspec = pl.BlockSpec(memory_space=pltpu.VMEM)
         aspec = pl.BlockSpec(memory_space=pl.ANY)

time: 42.9 us -> 42.8 us (level)
  no operation moved by 1% of the time
where the time goes in v5:
time: 42.8 us; the launch traced here: 42.7 us
  Pallas kernels  42 us (98%)
  between operations  0.65 us (2%)
    pallas_call x1, Pallas kernels, shards(): pl.pallas_call(functools.partial(kernel, (leaves, across, size, ups, coun...  41.4 us

profile of v5, /device:TPU:0, one launch (start us, length us, event | category | flops | bytes accessed | tf_op | source)
XLA Modules:
  0.0 42.7 jit_solution(4523240627758757412)
XLA Ops:
  0.6 41.4 %shard_map.309 = (f32[8,128]{1,0:T(8,128)S(1)}, f32[8,128]{1,0:T(8,128)S(1)}, f32[8,128]{1,0:T(8,128)S(1)}, f32[8,128]{1,0:T(8,128)S(1)}) custom-call(f32[8,128]{1,0:T(8,128)} %refs_0_.1, f32[8,128]{1,0:T(8,128)} %refs_1_.1, f32[8,128]{1,0:T(8,128)} %refs_2_.1, f32[8,128]{1,0:T(8,128)} %refs_3_.1, f32[128,128]{1,0:T(8,128)} %refs_4_.1, f32[128,128]{1,0:T(8,128)} %refs_5_.1, ...), custom_call_target="tpu_custom_call" | custom-call | tf_op jit(solution)/shard_map/pallas_call | solution.py:1069
  42.0 0.6 %shard_map.310 = (f32[8,128]{1,0:T(8,128)}, f32[8,128]{1,0:T(8,128)}, f32[8,128]{1,0:T(8,128)}, f32[8,128]{1,0:T(8,128)}) custom-call(f32[8,128]{1,0:T(8,128)S(1)} %get-tuple-element.8.refs_0_, f32[8,128]{1,0:T(8,128)S(1)} %get-tuple-element.9.refs_1_, f32[8,128]{1,0:T(8,128)S(1)} %get-tuple-element.10.refs_2_, f32[8,128]{1,0:T(8,128)S(1)} %get-tuple-element.11.refs_3_), custom_call_target="tpu_custom_call" | custom-call | tf_op jit(solution)/shard_map/pallas_call | solution.py:1079
